TPU v7x, 64 devices: a 2x2x8 block of a 4x4x8 slice. The times are simulated.
64 devices in a mesh: rep: 8 (over x, y, core), dp: 8 (over z).
Axes of the slice: x: 2, y: 2, z: 8, core: 2. Of those that a mesh axis runs over, the one named last changes fastest.
The devices are a block of a 4x4x8 slice.
Arguments:
- x: bfloat16 [64, 2048, 512], P(('rep', 'dp')), parts along dimension 0
- dy: bfloat16 [64, 2048, 512], P(('rep', 'dp')), parts along dimension 0
- w_gate: bfloat16 [2, 512, 3072], replicated
- w_up: bfloat16 [2, 512, 3072], replicated
- w_down: bfloat16 [2, 3072, 512], replicated
- m_w_gate: float32 [2, 512, 3072], P(None, 'dp')
- m_w_up: float32 [2, 512, 3072], P(None, 'dp')
- m_w_down: float32 [2, 3072, 512], P(None, 'dp')
- v_w_gate: float32 [2, 512, 3072], P(None, 'dp')
- v_w_up: float32 [2, 512, 3072], P(None, 'dp')
- v_w_down: float32 [2, 3072, 512], P(None, 'dp')
Outputs:
- output 1: bfloat16 [16, 512, 3072], P('rep'), parts along dimension 0
- output 2: bfloat16 [16, 512, 3072], P('rep'), parts along dimension 0
- output 3: bfloat16 [16, 3072, 512], P('rep'), parts along dimension 0
- output 4: float32 [16, 512, 3072], P('rep', 'dp'), parts along dimension 0
- output 5: float32 [16, 512, 3072], P('rep', 'dp'), parts along dimension 0
- output 6: float32 [16, 3072, 512], P('rep', 'dp'), parts along dimension 0
- output 7: float32 [16, 512, 3072], P('rep', 'dp'), parts along dimension 0
- output 8: float32 [16, 512, 3072], P('rep', 'dp'), parts along dimension 0
- output 9: float32 [16, 3072, 512], P('rep', 'dp'), parts along dimension 0
There are 8 independent parts. A program takes and returns all parts, laid end to end along the dimension named above; an argument that names none is the same for every part.
All inputs are finite; a program needn't handle non-finite values.
Results may differ from a plain program's by a relative error of at most 0.022.
Values are sent between devices in bfloat16 or wider.
A program may use at most 768 MiB of HBM per device.

v0:
```python
import jax
import jax.numpy as jnp
from jax import lax

NAMES = ("w_gate", "w_up", "w_down")


def matmul(a, w):
    return jnp.dot(a, w, preferred_element_type=jnp.float32).astype(jnp.bfloat16)


def normed(h):
    wide = h.astype(jnp.float32)
    scale = lax.rsqrt(jnp.mean(wide**2, -1, keepdims=True) + 1e-6)
    return (wide * scale).astype(jnp.bfloat16)


def layer(h, w):
    a = normed(h)
    gate = jnp.dot(a, w["w_gate"], preferred_element_type=jnp.float32)
    up = jnp.dot(a, w["w_up"], preferred_element_type=jnp.float32)
    return h + matmul((jax.nn.silu(gate) * up).astype(jnp.bfloat16), w["w_down"])


def adamw(w, m, v, g):
    m = 0.9 * m + 0.1 * g
    v = 0.95 * v + 0.05 * g * g
    step = m * lax.rsqrt(v + 1e-8) + 0.1 * w
    return (w - 0.02 * step).astype(jnp.bfloat16), m, v


def stack(weights, h):
    for number in range(weights["w_gate"].shape[0]):
        h = layer(h, {name: w[number] for name, w in weights.items()})
    return h


def solution(mesh):
    groups = mesh.shape["rep"]

    def step(x, dy, *arrays):
        weights, m, v = (arrays[i : i + 3] for i in (0, 3, 6))
        x, dy = (t.reshape(groups, -1, *t.shape[1:]) for t in (x, dy))

        def of_a_group(x, dy):
            _, back = jax.vjp(lambda w: stack(w, x), dict(zip(NAMES, weights, strict=True)))
            by_weights = back(dy)[0]
            gradients = [by_weights[name].astype(jnp.float32) for name in NAMES]
            new = [adamw(w.astype(jnp.float32), m, v, g) for w, m, v, g in zip(weights, m, v, gradients, strict=True)]
            return tuple(one[which] for which in range(3) for one in new)

        return tuple(t.reshape(-1, *t.shape[2:]) for t in jax.vmap(of_a_group)(x, dy))

    return step
```

profile of v0, /device:TPU:21, one launch (start us, length us, event | category | flops | bytes accessed | tf_op | source)
XLA Modules:
  0.0 864.9 jit_solution(13117925049907487861)
XLA Ops:
  9.5 3.9 copy
  13.4 13.7 %fusion.67 = f32[2048,3072]{1,0:T(8,128)} fusion(bf16[2,512,3072]{2,1,0:T(8,128)(2,1)} %param, bf16[1,2048,512]{2,1,0:T(8,128)(2,1)S(1)} %copy-done.1, f32[2048]{0:T(1024)S(1)} %add_rsqrt_fusion), kind=kOutput, calls=%fused_computation.79 | convolution fusion | flops 6445596672 | bytes 30416896 | tf_op jit(solution)/vmap(jvp())/dot_general | solution.py:20
  27.1 13.6 %fusion.65 = f32[2048,3072]{1,0:T(8,128)} fusion(bf16[2,512,3072]{2,1,0:T(8,128)(2,1)} %param.3, bf16[1,2048,512]{2,1,0:T(8,128)(2,1)S(1)} %copy-done.1, f32[2048]{0:T(1024)S(1)} %add_rsqrt_fusion), kind=kOutput, calls=%fused_computation.77 | convolution fusion | flops 6445596672 | bytes 30416896 | tf_op jit(solution)/vmap(jvp())/dot_general | solution.py:21
  40.7 21.8 %fusion.26 = bf16[2048,3072]{1,0:T(8,128)(2,1)} fusion(f32[2048,3072]{1,0:T(8,128)} %fusion.65, f32[2048,3072]{1,0:T(8,128)} %fusion.67), kind=kLoop, calls=%fused_computation.35 | loop fusion | flops 37748736 | bytes 62914560
  62.5 10.8 %fusion.51 = (f32[2048]{0:T(1024)S(1)}, bf16[1,1,2048,512]{2,3,1,0:T(8,128)(2,1)S(1)}) fusion(bf16[2048,3072]{1,0:T(8,128)(2,1)} %fusion.26, bf16[2,3072,512]{2,1,0:T(8,128)(2,1)} %param.4, bf16[1,2048,512]{1,2,0:T(8,128)(2,1)S(1)} %copy-done.5), kind=kOutput, calls=%fused_computation.62 | convolution fusion | flops 6447691776 | bytes 19931136 | tf_op jit(solution)/vmap(jvp())/dot_general | solution.py:9
  73.3 15.1 %fusion.56 = f32[2048,3072]{1,0:T(8,128)} fusion(bf16[2,512,3072]{2,1,0:T(8,128)(2,1)} %param, bf16[1,1,2048,512]{2,3,1,0:T(8,128)(2,1)S(1)} %get-tuple-element.10, f32[2048]{0:T(1024)S(1)} %bitcast.374), kind=kOutput, calls=%fused_computation.68 | convolution fusion | flops 6445596672 | bytes 30416896 | tf_op jit(solution)/vmap(jvp())/dot_general | solution.py:20
  88.4 13.9 %fusion.59 = f32[2048,3072]{1,0:T(8,128)} fusion(bf16[2,512,3072]{2,1,0:T(8,128)(2,1)} %param.3, bf16[1,1,2048,512]{2,3,1,0:T(8,128)(2,1)S(1)} %get-tuple-element.10, f32[2048]{0:T(1024)S(1)} %bitcast.375), kind=kOutput, calls=%fused_computation.71 | convolution fusion | flops 6445596672 | bytes 30416896 | tf_op jit(solution)/vmap(jvp())/dot_general | solution.py:21
  102.3 9.9 %convolution_convert_fusion.1 = bf16[2048,3072]{1,0:T(8,128)(2,1)} fusion(bf16[2,3072,512]{2,1,0:T(8,128)(2,1)S(1)} %bitcast.370, bf16[1,2048,512]{2,1,0:T(8,128)(2,1)S(1)} %copy-done.3), kind=kOutput, calls=%fused_computation.44 | convolution fusion | flops 6448742400 | bytes 17825792 | tf_op jit(solution)/vmap(transpose(jvp()))/dot_general | solution.py:9
  115.1 21.3 %fusion.6 = bf16[2048,3072]{1,0:T(8,128)(2,1)S(1)} fusion(f32[2048,3072]{1,0:T(8,128)} %fusion.56, f32[2048,3072]{1,0:T(8,128)} %fusion.59, bf16[2048,3072]{1,0:T(8,128)(2,1)} %convolution_convert_fusion.1), kind=kLoop, calls=%fused_computation.11 | loop fusion | flops 75497472 | bytes 75497472
  136.4 4.5 copy-done
  140.9 9.3 %fusion.80 = bf16[2048,512]{0,1:T(8,128)(2,1)} fusion(bf16[2048,3072]{1,0:T(8,128)(2,1)S(1)} %fusion.6, bf16[2,512,3072]{2,1,0:T(8,128)(2,1)} %param), kind=kOutput, calls=%fused_computation.86 | convolution fusion | flops 6442450944 | bytes 17825792 | tf_op jit(solution)/vmap(transpose(jvp()))/dot_general | solution.py:20
  150.1 20.8 %fusion.53 = (f32[2048]{0:T(1024)S(1)}, bf16[1,1,2048,512]{2,3,1,0:T(8,128)(2,1)}) fusion(bf16[1,1,2048,512]{2,3,1,0:T(8,128)(2,1)} %copy-done.7, bf16[2048,512]{0,1:T(8,128)(2,1)} %fusion.80, bf16[2,512,3072]{2,1,0:T(8,128)(2,1)} %param.3, bf16[2048,3072]{1,0:T(8,128)(2,1)} %convolution_convert_fusion.1, f32[2048,3072]{1,0:T(8,128)} %fusion.56), kind=kOutput, calls=%fused_computation.64 | convolution fusion | flops 6486489088 | bytes 47194112 | tf_op jit(solution)/vmap(transpose(jvp()))/dot_general | solution.py:21
  171.0 3.6 fusion.108
  175.9 11.6 %convolution_bitcast_fusion = f32[1,3072,512]{2,1,0:T(8,128)} fusion(bf16[2048,3072]{1,0:T(8,128)(2,1)} %fusion.26, bf16[2048,512]{0,1:T(8,128)(2,1)S(1)} %fusion.108), kind=kOutput, calls=%fused_computation.54 | convolution fusion | flops 6442450944 | bytes 20971520 | tf_op jit(solution)/vmap(transpose(jvp()))/dot_general | solution.py:9
  189.1 20.7 %fusion.35 = f32[1,3072,512]{2,1,0:T(8,128)} fusion(f32[2048,3072]{1,0:T(8,128)} %fusion.59, f32[2048,3072]{1,0:T(8,128)} %fusion.56, bf16[1,2048,512]{2,1,0:T(8,128)(2,1)S(1)} %copy-done.4), kind=kOutput, calls=%fused_computation.52 | convolution fusion | flops 6480199680 | bytes 58720256 | tf_op jit(solution)/vmap(transpose(jvp()))/dot_general | solution.py:9
  210.0 12.4 %convolution_convert_fusion = bf16[2048,3072]{1,0:T(8,128)(2,1)} fusion(bf16[2048,512]{0,1:T(8,128)(2,1)} %copy-done.8, bf16[2,3072,512]{2,1,0:T(8,128)(2,1)} %param.4), kind=kOutput, calls=%fused_computation.43 | convolution fusion | flops 6448742400 | bytes 17825792 | tf_op jit(solution)/vmap(transpose(jvp()))/dot_general | solution.py:9
  222.4 17.9 %fusion.44 = f32[1,512,3072]{2,1,0:T(8,128)} fusion(bf16[2048,3072]{1,0:T(8,128)(2,1)} %convolution_convert_fusion, f32[2048,3072]{1,0:T(8,128)} %fusion.67, bf16[1,2048,512]{1,2,0:T(8,128)(2,1)S(1)} %copy-done.6, f32[2048]{0:T(1024)S(1)} %copy-done.16), kind=kOutput, calls=%fused_computation.57 | convolution fusion | flops 6483345408 | bytes 46145536 | tf_op jit(solution)/vmap(transpose(jvp()))/dot_general | solution.py:21
  240.4 18.8 %fusion.41 = f32[1,512,3072]{2,1,0:T(8,128)} fusion(bf16[2048,3072]{1,0:T(8,128)(2,1)} %convolution_convert_fusion.1, f32[2048,3072]{1,0:T(8,128)} %fusion.56, bf16[1,1,2048,512]{2,3,1,0:T(8,128)(2,1)} %copy-done.7, f32[2048]{0:T(1024)S(1)} %bitcast.377), kind=kOutput, calls=%fused_computation.56 | convolution fusion | flops 6483345408 | bytes 46145536 | tf_op jit(solution)/vmap(transpose(jvp()))/dot_general | solution.py:21
  259.4 12.1 %convolution_bitcast_fusion.1 = f32[1,512,3072]{2,1,0:T(8,128)} fusion(bf16[2048,3072]{1,0:T(8,128)(2,1)} %copy-done, bf16[1,1,2048,512]{2,3,1,0:T(8,128)(2,1)} %copy-done.7, f32[2048]{0:T(1024)S(1)} %bitcast.378), kind=kOutput, calls=%fused_computation.55 | convolution fusion | flops 6445596672 | bytes 20979712 | tf_op jit(solution)/vmap(transpose(jvp()))/dot_general | solution.py:20
  271.6 25.3 %fusion.38 = f32[1,512,3072]{2,1,0:T(8,128)} fusion(f32[2048,3072]{1,0:T(8,128)} %fusion.67, f32[2048,3072]{1,0:T(8,128)} %fusion.65, bf16[2048,3072]{1,0:T(8,128)(2,1)} %convolution_convert_fusion, bf16[1,2048,512]{1,2,0:T(8,128)(2,1)S(1)} %copy-done.6, f32[2048]{0:T(1024)S(1)} %copy-done.16), kind=kOutput, calls=%fused_computation.53 | convolution fusion | flops 6514802688 | bytes 71311360 | tf_op jit(solution)/vmap(transpose(jvp()))/dot_general | solution.py:20
  300.0 36.8 %reduce-scatter.27.cloned.1.call-done = f32[1,384,512]{2,1,0:T(8,128)} async-done(((f32[1,3072,512]{2,1,0:T(8,128)}), f32[1,384,512]{2,1,0:T(8,128)}) %reduce-scatter.27.cloned.1.call-update) | async-done | bytes 786448
  338.0 3.9 fusion.144
  342.1 68.1 %reduce-scatter.25.cloned.1.call-done = f32[1,64,3072]{2,1,0:T(8,128)} async-done(((f32[1,512,3072]{2,1,0:T(8,128)}), f32[1,64,3072]{2,1,0:T(8,128)}) %reduce-scatter.25.cloned.1.call-update) | async-done | bytes 786448
  411.4 71.5 %reduce-scatter.23.cloned.1.call-done = f32[1,64,3072]{2,1,0:T(8,128)} async-done(((f32[1,512,3072]{2,1,0:T(8,128)}), f32[1,64,3072]{2,1,0:T(8,128)}) %reduce-scatter.23.cloned.1.call-update) | async-done | bytes 786448
  484.1 3.9 fusion.145
  488.1 68.0 %reduce-scatter.19.cloned.1.call-done = f32[1,64,3072]{2,1,0:T(8,128)} async-done(((f32[1,512,3072]{2,1,0:T(8,128)}), f32[1,64,3072]{2,1,0:T(8,128)}) %reduce-scatter.19.cloned.1.call-update) | async-done | bytes 786448
  557.3 72.1 %reduce-scatter.21.cloned.1.call-done = f32[1,64,3072]{2,1,0:T(8,128)} async-done(((f32[1,512,3072]{2,1,0:T(8,128)}), f32[1,64,3072]{2,1,0:T(8,128)}) %reduce-scatter.21.cloned.1.call-update) | async-done | bytes 786448
  630.6 3.9 fusion.146
  634.6 66.1 %all-gather.14.cloned.1.call-done = bf16[1,2,3072,512]{3,2,1,0:T(8,128)(2,1)} async-done(((bf16[1,2,384,512]{3,2,1,0:T(8,128)(2,1)}), bf16[1,2,3072,512]{3,2,1,0:T(8,128)(2,1)}) %all-gather.14.cloned.1.call-update) | async-done | bytes 6291472 | tf_op jit(solution)/reshape | solution.py:52
  700.7 71.8 %all-gather.12.cloned.1.call-done = bf16[1,2,512,3072]{3,2,1,0:T(8,128)(2,1)} async-done(((bf16[1,2,64,3072]{3,2,1,0:T(8,128)(2,1)}), bf16[1,2,512,3072]{3,2,1,0:T(8,128)(2,1)}) %all-gather.12.cloned.1.call-update) | async-done | bytes 6291472 | tf_op jit(solution)/reshape | solution.py:52
  772.5 71.8 %all-gather.10.cloned.1.call-done = bf16[1,2,512,3072]{3,2,1,0:T(8,128)(2,1)} async-done(((bf16[1,2,64,3072]{3,2,1,0:T(8,128)(2,1)}), bf16[1,2,512,3072]{3,2,1,0:T(8,128)(2,1)}) %all-gather.10.cloned.1.call-update) | async-done | bytes 6291472 | tf_op jit(solution)/reshape | solution.py:52
  844.3 6.6 copy.5
  (79 shorter events, 24.5 us)
Async XLA Ops:
  7.2 6.2 copy-start.1
  7.2 291.6 %reduce-scatter.29.cloned.1.call-start = ((), (), s32[]{:S(2)}) async-start(), calls=%async_computation.14 | async-start | bytes 7077888
  13.4 13.7 %copy-start.15 = (f32[2048]{0:T(1024)}, f32[2048]{0:T(1024)S(1)}, u32[]{:S(2)}) copy-start(f32[2048]{0:T(1024)S(1)} %add_rsqrt_fusion) | copy-start | bytes 24580
  40.7 21.8 %copy-start.5 = (bf16[1,2048,512]{1,2,0:T(8,128)(2,1)S(1)}, bf16[1,2048,512]{1,2,0:T(8,128)(2,1)}, u32[]{:S(2)}) copy-start(bf16[1,2048,512]{1,2,0:T(8,128)(2,1)} %copy) | copy-start | bytes 6291460
  73.3 15.1 %copy-start.7 = (bf16[1,1,2048,512]{2,3,1,0:T(8,128)(2,1)}, bf16[1,1,2048,512]{2,3,1,0:T(8,128)(2,1)S(1)}, u32[]{:S(2)}) copy-start(bf16[1,1,2048,512]{2,3,1,0:T(8,128)(2,1)S(1)} %get-tuple-element.10) | copy-start | bytes 6291460
  73.3 29.0 %slice-start.2 = ((s8[6291456]{0:T(1024)(128)(4,1)}), s8[4194304]{0:T(1024)(128)(4,1)S(1)}, s32[]{:S(2)}) async-start(s8[6291456]{0:T(1024)(128)(4,1)} %bitcast.369), calls=%async_computation.17 | async-start | bytes 8388608
  88.4 13.9 %copy-start.3 = (bf16[1,2048,512]{2,1,0:T(8,128)(2,1)S(1)}, bf16[1,2048,512]{2,1,0:T(8,128)(2,1)}, u32[]{:S(2)}) copy-start(bf16[1,2048,512]{2,1,0:T(8,128)(2,1)} %param.5) | copy-start | bytes 6291460
  88.4 13.9 %slice-start.3 = ((s8[6291456]{0:T(1024)(128)(4,1)}), s8[2097152]{0:T(1024)(128)(4,1)S(1)}, s32[]{:S(2)}) async-start(s8[6291456]{0:T(1024)(128)(4,1)} %bitcast.369), calls=%async_computation.18 | async-start | bytes 4194304
  136.4 4.5 copy-start
  174.6 1.3 copy-start.8
  187.5 1.6 copy-start.4
  187.5 149.2 %reduce-scatter.27.cloned.1.call-start = ((), (), s32[]{:S(2)}) async-start(), calls=%async_computation.13 | async-start | bytes 7077888
  209.9 12.5 %copy-start.6 = (bf16[1,2048,512]{1,2,0:T(8,128)(2,1)S(1)}, bf16[1,2048,512]{1,2,0:T(8,128)(2,1)}, u32[]{:S(2)}) copy-start(bf16[1,2048,512]{1,2,0:T(8,128)(2,1)} %copy) | copy-start | bytes 6291460
  209.9 12.5 %copy-start.16 = (f32[2048]{0:T(1024)S(1)}, f32[2048]{0:T(1024)}, u32[]{:S(2)}) copy-start(f32[2048]{0:T(1024)} %copy-done.15) | copy-start | bytes 24580
  209.9 200.3 %reduce-scatter.25.cloned.1.call-start = ((), (), s32[]{:S(2)}) async-start(), calls=%async_computation.12 | async-start | bytes 7077888
  240.3 242.6 %reduce-scatter.23.cloned.1.call-start = ((), (), s32[]{:S(2)}) async-start(), calls=%async_computation.11 | async-start | bytes 7077888
  259.3 296.9 %reduce-scatter.19.cloned.1.call-start = ((), (), s32[]{:S(2)}) async-start(), calls=%async_computation.9 | async-start | bytes 7077888
  271.5 357.9 %reduce-scatter.21.cloned.1.call-start = ((), (), s32[]{:S(2)}) async-start(), calls=%async_computation.10 | async-start | bytes 7077888
  296.9 0.7 copy-start.17
  296.9 41.1 %copy-start.9 = (f32[2,384,512]{2,1,0:T(8,128)S(1)}, f32[2,384,512]{2,1,0:T(8,128)}, u32[]{:S(2)}) copy-start(f32[2,384,512]{2,1,0:T(8,128)} %param.10) | copy-start | bytes 4718596
  296.9 41.1 %copy-start.10 = (f32[2,384,512]{2,1,0:T(8,128)S(1)}, f32[2,384,512]{2,1,0:T(8,128)}, u32[]{:S(2)}) copy-start(f32[2,384,512]{2,1,0:T(8,128)} %param.9) | copy-start | bytes 4718596
  297.0 403.7 %all-gather.14.cloned.1.call-start = ((), (), s32[]{:S(2)}) async-start(), calls=%async_computation.8 | async-start | bytes 7077888 | tf_op jit(solution)/reshape | solution.py:52
  341.9 142.2 %copy-start.11 = (f32[2,64,3072]{2,1,0:T(8,128)S(1)}, f32[2,64,3072]{2,1,0:T(8,128)}, u32[]{:S(2)}) copy-start(f32[2,64,3072]{2,1,0:T(8,128)} %param.8) | copy-start | bytes 4718596
  341.9 142.2 %copy-start.12 = (f32[2,64,3072]{2,1,0:T(8,128)S(1)}, f32[2,64,3072]{2,1,0:T(8,128)}, u32[]{:S(2)}) copy-start(f32[2,64,3072]{2,1,0:T(8,128)} %param.7) | copy-start | bytes 4718596
  342.0 430.5 %all-gather.12.cloned.1.call-start = ((), (), s32[]{:S(2)}) async-start(), calls=%async_computation.7 | async-start | bytes 7077888 | tf_op jit(solution)/reshape | solution.py:52
  488.0 142.6 %copy-start.13 = (f32[2,64,3072]{2,1,0:T(8,128)S(1)}, f32[2,64,3072]{2,1,0:T(8,128)}, u32[]{:S(2)}) copy-start(f32[2,64,3072]{2,1,0:T(8,128)} %param.6) | copy-start | bytes 4718596
  488.0 142.6 %copy-start.14 = (f32[2,64,3072]{2,1,0:T(8,128)S(1)}, f32[2,64,3072]{2,1,0:T(8,128)}, u32[]{:S(2)}) copy-start(f32[2,64,3072]{2,1,0:T(8,128)} %param.1) | copy-start | bytes 4718596
  488.1 356.2 %all-gather.10.cloned.1.call-start = ((), (), s32[]{:S(2)}) async-start(), calls=%async_computation.6 | async-start | bytes 7077888 | tf_op jit(solution)/reshape | solution.py:52
  844.3 6.6 copy-start.2
  844.3 9.8 %slice-start = ((s8[6291456]{0:T(1024)(128)(4,1)}), s8[4194304]{0:T(1024)(128)(4,1)S(1)}, s32[]{:S(2)}) async-start(s8[6291456]{0:T(1024)(128)(4,1)} %bitcast.364), calls=%async_computation.15 | async-start | bytes 8388608
  850.9 4.5 slice-start.1
Sparse Core Ops, SparseCore 0:
  187.7 76.2 reduce-scatter.28
  266.3 70.4 reduce-scatter.26
  339.7 70.4 reduce-scatter.24
  412.4 70.4 reduce-scatter.22
  485.7 70.4 reduce-scatter.18
  558.9 70.4 reduce-scatter.20
  631.0 69.6 all-gather.13
  702.8 69.5 all-gather.11
  774.6 69.5 all-gather.9
where the time goes:
time: 873 us; the launch traced here: 865 us
  waiting for transfers between devices  527 us (60%)
  matrix products  226 us (26%)
  other arithmetic  67.6 us (8%)
  local copies, waits for them, and re-layouts  29.1 us (3%)
  between operations  15 us (2%)
    unnamed x15, waiting for transfers between devices  317 us
    reshape x3, waiting for transfers between devices, step(): t.reshape(-1, *t.shape[2:])  210 us
    dot_general x5, matrix products, layer(): up = jnp.dot(a, w['w_up'], preferred_element_type=jnp.float32)  85 us
    dot_general x5, matrix products, layer(): gate = jnp.dot(a, w['w_gate'], preferred_element_type=jnp.float32)  75.4 us
    dot_general x5, matrix products, matmul(): jnp.dot(a, w, preferred_element_type=jnp.float32).astype(jnp.bfloat16)  65.4 us
    unnamed x5, other arithmetic  46.6 us
    unnamed x49, local copies, waits for them, and re-layouts  28.5 us
  transfers between devices with their start and end apart: 9, of which 8 were waited for; matrix products, arithmetic and copies ran while one was open for 15% of the time, Pallas kernels for 0%

commit v1 on v0

v1 whole, which is shorter than its diff:
```python
import jax
import jax.numpy as jnp
from jax import lax
from jax.sharding import PartitionSpec as P

F32 = jnp.float32
BF16 = jnp.bfloat16


def dot(a, b, dims=((1,), (0,))):
    return lax.dot_general(a, b, (dims, ((), ())), preferred_element_type=F32)


def normed(h):
    wide = h.astype(F32)
    scale = lax.rsqrt(jnp.mean(wide**2, -1, keepdims=True) + 1e-6)
    return (wide * scale).astype(BF16), scale


def adamw(w, m, v, g):
    m = 0.9 * m + 0.1 * g
    v = 0.95 * v + 0.05 * g * g
    step = m * lax.rsqrt(v + 1e-8) + 0.1 * w
    return (w - 0.02 * step).astype(BF16), m, v


def device_step(x, dy, w_gate, w_up, w_down, *moments):
    m, v = moments[:3], moments[3:]
    layers = w_gate.shape[0]
    me = lax.axis_index("dp")
    h = x[0]
    saved = []
    for n in range(layers):
        a, scale = normed(h)
        gate = dot(a, w_gate[n])
        up = dot(a, w_up[n])
        sig = jax.nn.sigmoid(gate)
        p = (gate * sig * up).astype(BF16)
        saved.append((h, a, scale, gate, up, sig, p))
        if n < layers - 1:
            h = h + dot(p, w_down[n]).astype(BF16)
    ct = dy[0]
    sums = [None] * layers
    for n in reversed(range(layers)):
        h, a, scale, gate, up, sig, p = saved[n]
        d_down = dot(p, ct, ((0,), (0,))).astype(BF16)
        dp = dot(ct, w_down[n], ((1,), (1,))).astype(BF16).astype(F32)
        d_up_in = (dp * gate * sig).astype(BF16)
        d_gate_in = (dp * up * (sig + gate * sig * (1 - sig))).astype(BF16)
        d_gate = dot(a, d_gate_in, ((0,), (0,))).astype(BF16)
        d_up = dot(a, d_up_in, ((0,), (0,))).astype(BF16)
        sums[n] = [lax.psum_scatter(g, "dp", scatter_dimension=0, tiled=True) for g in (d_gate, d_up, d_down)]
        if n > 0:
            da = dot(d_gate_in, w_gate[n], ((1,), (1,))).astype(BF16) + dot(d_up_in, w_up[n], ((1,), (1,))).astype(BF16)
            da = da.astype(F32)
            wide = h.astype(F32)
            inner = jnp.mean(da * wide, -1, keepdims=True)
            ct = ct + (da * scale - wide * (scale**3 * inner)).astype(BF16)
    new = []
    for i, w in enumerate((w_gate, w_up, w_down)):
        rows = m[i].shape[1]
        own = lax.dynamic_slice_in_dim(w, me * rows, rows, 1).astype(F32)
        g = jnp.stack([sums[n][i] for n in range(layers)]).astype(F32)
        new.append(adamw(own, m[i], v[i], g))
    gathered = tuple(lax.all_gather(one[0], "dp", axis=1, tiled=True) for one in new)
    return gathered + tuple(one[which] for which in (1, 2) for one in new)


def solution(mesh):
    whole, rows, seq = P(None, None, None), P(None, "dp", None), P(("rep", "dp"), None, None)
    return jax.shard_map(
        device_step,
        mesh=mesh,
        in_specs=(seq, seq) + (whole,) * 3 + (rows,) * 6,
        out_specs=(P("rep", None, None),) * 3 + (P("rep", "dp", None),) * 6,
        check_vma=False,
    )
```

time: 873 us -> 673 us (0.77)
  waiting for transfers between devices: 527 us -> 373 us
  other arithmetic: 67.6 us -> 14.2 us
  matrix products: 226 us -> 237 us
    unnamed x15 -> x9, waiting for transfers between devices: 317 us -> 0.48 us
    all_gather x0 -> x3, waiting for transfers between devices: none -> 214 us  [device_step(): lax.all_gather(one[0], 'dp', axis=1, tiled=True)]
    reshape x3 -> x0, waiting for transfers between devices: 210 us -> none  [step(): t.reshape(-1, *t.shape[2:])]
    reduce_scatter x0 -> x6, waiting for transfers between devices: none -> 159 us  [device_step(): lax.psum_scatter(g, 'dp', scatter_dimension=0, tiled=True)]
    unnamed x5 -> x1, other arithmetic: 46.6 us -> 0.01 us
    convert_element_type x0 -> x3, other arithmetic: none -> 12.4 us  [adamw(): return ((w - 0.02 * step).astype(BF16), m, v)]
    reshape x3 -> x0, other arithmetic: 11.7 us -> none  [step(): t.reshape(-1, *t.shape[2:])]
    dot_general x15, matrix products: 226 us -> 237 us  [dot(): return lax.dot_general(a, b, (dims, ((), ())), preferred_element_type=F32)]
  transfers between devices with their start and end apart: 9 -> 9, of which waited for: 8 -> 7; matrix products, arithmetic and copies ran while one was open for 15% -> 17% of each run, Pallas kernels for 0% -> 0%
where the time goes in v1:
time: 673 us; the launch traced here: 665 us
  waiting for transfers between devices  373 us (55%)
  matrix products  237 us (35%)
  local copies, waits for them, and re-layouts  26.9 us (4%)
  between operations  14.5 us (2%)
  other arithmetic  14.2 us (2%)
    dot_general x15, matrix products, dot(): return lax.dot_general(a, b, (dims, ((), ())), preferred_element_type=F32)  237 us
    all_gather x3, waiting for transfers between devices, device_step(): lax.all_gather(one[0], 'dp', axis=1, tiled=True)  214 us
    reduce_scatter x6, waiting for transfers between devices, device_step(): lax.psum_scatter(g, 'dp', scatter_dimension=0, tiled=True)  159 us
    unnamed x41, local copies, waits for them, and re-layouts  26.9 us
  transfers between devices with their start and end apart: 9, of which 7 were waited for; matrix products, arithmetic and copies ran while one was open for 17% of the time, Pallas kernels for 0%

profile of v1, /device:TPU:21, one launch (start us, length us, event | category | flops | bytes accessed | tf_op | source)
XLA Modules:
  0.0 665.5 jit_solution(3668506652399066670)
XLA Ops:
  7.3 2.9 copy.20
  10.7 4.2 copy.21
  14.8 12.0 %convolution_convert_fusion.1 = bf16[2048,3072]{1,0:T(8,128)(2,1)} fusion(bf16[2,3072,512]{2,1,0:T(8,128)(2,1)} %param.15, bf16[1,2048,512]{2,1,0:T(8,128)(2,1)} %param.12), kind=kOutput, calls=%fused_computation.22 | convolution fusion | flops 6448742400 | bytes 17825792 | tf_op jit(solution)/shard_map/dot_general | solution.py:11
  26.8 13.7 %fusion.44 = f32[2048,3072]{1,0:T(8,128)} fusion(bf16[2,512,3072]{2,1,0:T(8,128)(2,1)} %param.13, bf16[1,2048,512]{2,1,0:T(8,128)(2,1)S(1)} %copy-done.4, f32[2048]{0:T(1024)S(1)} %add_rsqrt_fusion.1), kind=kOutput, calls=%fused_computation.57 | convolution fusion | flops 6445596672 | bytes 30416896 | tf_op jit(solution)/shard_map/dot_general | solution.py:11
  40.5 24.5 %multiply_convert_fusion.1 = (bf16[2048,3072]{1,0:T(8,128)(2,1)}, f32[2048,3072]{1,0:T(8,128)}) fusion(f32[2048,3072]{1,0:T(8,128)} %fusion.44, bf16[2,512,3072]{2,1,0:T(8,128)(2,1)} %param.14, bf16[1,2048,512]{2,1,0:T(8,128)(2,1)} %param.11, f32[2048]{0:T(1024)S(1)} %add_rsqrt_fusion.1), kind=kOutput, calls=%fused_computation.14 | convolution fusion | flops 6483345408 | bytes 68165632 | tf_op jit(solution)/shard_map/dot_general | solution.py:11
  65.0 11.2 %fusion.28 = (f32[2048]{0:T(1024)S(1)}, bf16[2048,512]{0,1:T(8,128)(2,1)S(1)}) fusion(bf16[2048,3072]{1,0:T(8,128)(2,1)} %get-tuple-element.20, bf16[2,3072,512]{2,1,0:T(8,128)(2,1)} %param.15, bf16[1,2048,512]{1,2,0:T(8,128)(2,1)S(1)} %copy.20), kind=kOutput, calls=%fused_computation.40 | convolution fusion | flops 6447691776 | bytes 19931136 | tf_op jit(solution)/shard_map/dot_general | solution.py:11
  76.2 14.4 %fusion.37 = f32[2048,3072]{1,0:T(8,128)} fusion(bf16[2,512,3072]{2,1,0:T(8,128)(2,1)} %param.14, bf16[2048,512]{0,1:T(8,128)(2,1)S(1)} %get-tuple-element.23, f32[2048]{0:T(1024)S(1)} %add_rsqrt_fusion), kind=kOutput, calls=%fused_computation.50 | convolution fusion | flops 6445596672 | bytes 30416896 | tf_op jit(solution)/shard_map/dot_general | solution.py:11
  90.6 32.4 %fusion.3 = (bf16[2048,3072]{1,0:T(8,128)(2,1)}, bf16[2048,3072]{1,0:T(8,128)(2,1)}, f32[2048,3072]{1,0:T(8,128)}) fusion(bf16[2048,3072]{1,0:T(8,128)(2,1)} %convolution_convert_fusion.1, f32[2048,3072]{1,0:T(8,128)} %fusion.37, bf16[2,512,3072]{2,1,0:T(8,128)(2,1)} %param.13, bf16[2048,512]{0,1:T(8,128)(2,1)S(1)} %get-tuple-element.23, ...), kind=kOutput, calls=%fused_computation.7 | convolution fusion | flops 6533677056 | bytes 93331456 | tf_op jit(solution)/shard_map/dot_general | solution.py:11
  123.0 10.9 %fusion.53 = bf16[2048,512]{0,1:T(8,128)(2,1)S(1)} fusion(bf16[2048,3072]{1,0:T(8,128)(2,1)} %get-tuple-element.18, bf16[2,512,3072]{2,1,0:T(8,128)(2,1)} %param.14), kind=kOutput, calls=%fused_computation.64 | convolution fusion | flops 6443499520 | bytes 17825792 | tf_op jit(solution)/shard_map/dot_general | solution.py:11
  133.9 8.9 %fusion.30 = (f32[2048]{0:T(1024)S(1)}, bf16[2048,512]{0,1:T(8,128)(2,1)S(1)}) fusion(bf16[2048,512]{0,1:T(8,128)(2,1)S(1)} %get-tuple-element.23, bf16[2048,512]{0,1:T(8,128)(2,1)S(1)} %fusion.53, bf16[2048,3072]{1,0:T(8,128)(2,1)S(1)} %copy-done.15, bf16[2,512,3072]{2,1,0:T(8,128)(2,1)} %param.13), kind=kOutput, calls=%fused_computation.42 | convolution fusion | flops 6448740352 | bytes 22028288 | tf_op jit(solution)/shard_map/dot_general | solution.py:11
  145.6 11.0 %convolution_convert_fusion.2 = bf16[3072,512]{1,0:T(8,128)(2,1)} fusion(bf16[2048,3072]{1,0:T(8,128)(2,1)} %get-tuple-element.20, bf16[2048,512]{0,1:T(8,128)(2,1)S(1)} %fusion.72), kind=kOutput, calls=%fused_computation.32 | convolution fusion | flops 6444023808 | bytes 17825792 | tf_op jit(solution)/shard_map/dot_general | solution.py:11
  156.7 1.5 copy-done.5
  158.2 19.9 %fusion.20 = bf16[3072,512]{1,0:T(8,128)(2,1)} fusion(f32[2048,3072]{1,0:T(8,128)} %fusion.37, f32[2048,3072]{1,0:T(8,128)} %get-tuple-element.24, bf16[1,2048,512]{2,1,0:T(8,128)(2,1)S(1)} %copy-done.5), kind=kOutput, calls=%fused_computation.31 | convolution fusion | flops 6481772544 | bytes 55574528 | tf_op jit(solution)/shard_map/dot_general | solution.py:11
  178.2 11.9 %convolution_convert_fusion = bf16[2048,3072]{1,0:T(8,128)(2,1)} fusion(bf16[2048,512]{0,1:T(8,128)(2,1)} %copy-done.8, bf16[2,3072,512]{2,1,0:T(8,128)(2,1)} %param.15), kind=kOutput, calls=%fused_computation.21 | convolution fusion | flops 6448742400 | bytes 17825792 | tf_op jit(solution)/shard_map/dot_general | solution.py:11
  190.1 17.4 %fusion.17 = bf16[512,3072]{1,0:T(8,128)(2,1)} fusion(f32[2048,3072]{1,0:T(8,128)} %fusion.44, bf16[2048,3072]{1,0:T(8,128)(2,1)} %convolution_convert_fusion, bf16[1,2048,512]{1,2,0:T(8,128)(2,1)S(1)} %copy-done.1, f32[2048]{0:T(1024)S(1)} %copy-done.14), kind=kOutput, calls=%fused_computation.30 | convolution fusion | flops 6491209728 | bytes 42999808 | tf_op jit(solution)/shard_map/dot_general | solution.py:11
  207.7 13.2 %convolution_convert_fusion.3 = bf16[512,3072]{1,0:T(8,128)(2,1)} fusion(bf16[2048,3072]{1,0:T(8,128)(2,1)} %get-tuple-element.18, bf16[2048,512]{0,1:T(8,128)(2,1)} %copy-done.6, f32[2048]{0:T(1024)S(1)} %add_rsqrt_fusion), kind=kOutput, calls=%fused_computation.33 | convolution fusion | flops 6447169536 | bytes 17833984 | tf_op jit(solution)/shard_map/dot_general | solution.py:11
  221.0 24.6 %fusion.21 = bf16[512,3072]{1,0:T(8,128)(2,1)} fusion(f32[2048,3072]{1,0:T(8,128)} %get-tuple-element.21, bf16[2048,3072]{1,0:T(8,128)(2,1)} %convolution_convert_fusion, f32[2048,3072]{1,0:T(8,128)} %fusion.44, bf16[1,2048,512]{1,2,0:T(8,128)(2,1)S(1)} %copy-done.1, f32[2048]{0:T(1024)S(1)} %copy-done.14), kind=kOutput, calls=%fused_computation.35 | convolution fusion | flops 6516375552 | bytes 68165632 | tf_op jit(solution)/shard_map/dot_general | solution.py:11
  245.7 1.5 copy-done.7
  247.2 10.8 %convolution_convert_fusion.4 = bf16[512,3072]{1,0:T(8,128)(2,1)} fusion(bf16[2048,3072]{1,0:T(8,128)(2,1)} %get-tuple-element.19, bf16[2048,512]{0,1:T(8,128)(2,1)S(1)} %copy-done.7, f32[2048]{0:T(1024)S(1)} %add_rsqrt_fusion), kind=kOutput, calls=%fused_computation.34 | convolution fusion | flops 6447169536 | bytes 17833984 | tf_op jit(solution)/shard_map/dot_general | solution.py:11
  259.8 3.8 fusion.87
  263.8 28.2 %reduce-scatter.11.cloned.1.call-done = bf16[64,3072]{1,0:T(8,128)(2,1)} async-done(((bf16[512,3072]{1,0:T(8,128)(2,1)}), bf16[64,3072]{1,0:T(8,128)(2,1)}) %reduce-scatter.11.cloned.1.call-update) | async-done | bytes 393232 | tf_op jit(solution)/shard_map/reduce_scatter | solution.py:52
  291.9 45.1 %reduce-scatter.13.cloned.1.call-done = bf16[64,3072]{1,0:T(8,128)(2,1)} async-done(((bf16[512,3072]{1,0:T(8,128)(2,1)}), bf16[64,3072]{1,0:T(8,128)(2,1)}) %reduce-scatter.13.cloned.1.call-update) | async-done | bytes 393232 | tf_op jit(solution)/shard_map/reduce_scatter | solution.py:52
  337.0 4.9 fusion.83
  342.0 40.2 %reduce-scatter.7.cloned.1.call-done = bf16[64,3072]{1,0:T(8,128)(2,1)} async-done(((bf16[512,3072]{1,0:T(8,128)(2,1)}), bf16[64,3072]{1,0:T(8,128)(2,1)}) %reduce-scatter.7.cloned.1.call-update) | async-done | bytes 393232 | tf_op jit(solution)/shard_map/reduce_scatter | solution.py:52
  382.2 45.1 %reduce-scatter.9.cloned.1.call-done = bf16[64,3072]{1,0:T(8,128)(2,1)} async-done(((bf16[512,3072]{1,0:T(8,128)(2,1)}), bf16[64,3072]{1,0:T(8,128)(2,1)}) %reduce-scatter.9.cloned.1.call-update) | async-done | bytes 393232 | tf_op jit(solution)/shard_map/reduce_scatter | solution.py:52
  427.4 3.7 fusion.79
  431.1 69.9 %all-gather.8.cloned.1.call-done = bf16[2,3072,512]{2,1,0:T(8,128)(2,1)} async-done(((bf16[2,384,512]{2,1,0:T(8,128)(2,1)}), bf16[2,3072,512]{2,1,0:T(8,128)(2,1)}) %all-gather.8.cloned.1.call-update) | async-done | bytes 6291472 | tf_op jit(solution)/shard_map/all_gather | solution.py:65
  501.0 71.8 %all-gather.6.cloned.1.call-done = bf16[2,512,3072]{2,1,0:T(8,128)(2,1)} async-done(((bf16[2,64,3072]{2,1,0:T(8,128)(2,1)}), bf16[2,512,3072]{2,1,0:T(8,128)(2,1)}) %all-gather.6.cloned.1.call-update) | async-done | bytes 6291472 | tf_op jit(solution)/shard_map/all_gather | solution.py:65
  572.8 71.8 %all-gather.4.cloned.1.call-done = bf16[2,512,3072]{2,1,0:T(8,128)(2,1)} async-done(((bf16[2,64,3072]{2,1,0:T(8,128)(2,1)}), bf16[2,512,3072]{2,1,0:T(8,128)(2,1)}) %all-gather.4.cloned.1.call-update) | async-done | bytes 6291472 | tf_op jit(solution)/shard_map/all_gather | solution.py:65
  644.6 6.6 copy.25
  651.3 3.2 copy.26
  655.8 2.7 copy.27
  (60 shorter events, 7.3 us)
Async XLA Ops:
  7.2 250.9 %reduce-scatter.15.cloned.1.call-start = ((), (), s32[]{:S(2)}) async-start(), calls=%async_computation.12 | async-start | bytes 3538944 | tf_op jit(solution)/shard_map/reduce_scatter | solution.py:52
  10.2 54.8 %copy-start = (bf16[1,2048,512]{1,2,0:T(8,128)(2,1)}, bf16[1,2048,512]{1,2,0:T(8,128)(2,1)S(1)}, u32[]{:S(2)}) copy-start(bf16[1,2048,512]{1,2,0:T(8,128)(2,1)S(1)} %copy.20) | copy-start | bytes 6291460
  10.7 29.8 %copy-start.13 = (f32[2048]{0:T(1024)}, f32[2048]{0:T(1024)S(1)}, u32[]{:S(2)}) copy-start(f32[2048]{0:T(1024)S(1)} %add_rsqrt_fusion.1) | copy-start | bytes 24580
  14.8 12.0 %copy-start.4 = (bf16[1,2048,512]{2,1,0:T(8,128)(2,1)S(1)}, bf16[1,2048,512]{2,1,0:T(8,128)(2,1)}, u32[]{:S(2)}) copy-start(bf16[1,2048,512]{2,1,0:T(8,128)(2,1)} %param.11) | copy-start | bytes 6291460
  76.2 66.7 %copy-start.6 = (bf16[2048,512]{0,1:T(8,128)(2,1)}, bf16[2048,512]{0,1:T(8,128)(2,1)S(1)}, u32[]{:S(2)}) copy-start(bf16[2048,512]{0,1:T(8,128)(2,1)S(1)} %get-tuple-element.23) | copy-start | bytes 6291460
  123.0 11.0 %copy-start.15 = (bf16[2048,3072]{1,0:T(8,128)(2,1)S(1)}, bf16[2048,3072]{1,0:T(8,128)(2,1)}, u32[]{:S(2)}) copy-start(bf16[2048,3072]{1,0:T(8,128)(2,1)} %get-tuple-element.19) | copy-start | bytes 37748740
  133.9 8.9 %copy-start.2 = (bf16[1,2048,512]{1,2,0:T(8,128)(2,1)S(1)}, bf16[1,2048,512]{1,2,0:T(8,128)(2,1)}, u32[]{:S(2)}) copy-start(bf16[1,2048,512]{1,2,0:T(8,128)(2,1)} %copy.21) | copy-start | bytes 6291460
  144.3 1.3 copy-start.8
  156.6 1.6 copy-start.5
  156.6 101.5 %reduce-scatter.17.cloned.1.call-start = ((), (), s32[]{:S(2)}) async-start(), calls=%async_computation.13 | async-start | bytes 3538944 | tf_op jit(solution)/shard_map/reduce_scatter | solution.py:52
  178.1 12.0 %copy-start.1 = (bf16[1,2048,512]{1,2,0:T(8,128)(2,1)S(1)}, bf16[1,2048,512]{1,2,0:T(8,128)(2,1)}, u32[]{:S(2)}) copy-start(bf16[1,2048,512]{1,2,0:T(8,128)(2,1)} %copy-done) | copy-start | bytes 6291460
  178.1 12.0 %copy-start.14 = (f32[2048]{0:T(1024)S(1)}, f32[2048]{0:T(1024)}, u32[]{:S(2)}) copy-start(f32[2048]{0:T(1024)} %copy-done.13) | copy-start | bytes 24580
  178.1 113.8 %reduce-scatter.11.cloned.1.call-start = ((), (), s32[]{:S(2)}) async-start(), calls=%async_computation.9 | async-start | bytes 3538944 | tf_op jit(solution)/shard_map/reduce_scatter | solution.py:52
  207.6 129.4 %reduce-scatter.13.cloned.1.call-start = ((), (), s32[]{:S(2)}) async-start(), calls=%async_computation.10 | async-start | bytes 3538944 | tf_op jit(solution)/shard_map/reduce_scatter | solution.py:52
  220.9 161.3 %reduce-scatter.7.cloned.1.call-start = ((), (), s32[]{:S(2)}) async-start(), calls=%async_computation.6 | async-start | bytes 3538944 | tf_op jit(solution)/shard_map/reduce_scatter | solution.py:52
  245.6 1.6 copy-start.7
  245.7 181.7 %reduce-scatter.9.cloned.1.call-start = ((), (), s32[]{:S(2)}) async-start(), calls=%async_computation.7 | async-start | bytes 3538944 | tf_op jit(solution)/shard_map/reduce_scatter | solution.py:52
  257.9 1.4 copy-start.9
  257.9 1.9 copy-start.10
  258.0 243.0 %all-gather.8.cloned.1.call-start = ((), (), s32[]{:S(2)}) async-start(), calls=%async_computation.14 | async-start | bytes 7077888 | tf_op jit(solution)/shard_map/all_gather | solution.py:65
  263.7 309.1 %all-gather.6.cloned.1.call-start = ((), (), s32[]{:S(2)}) async-start(), calls=%async_computation.11 | async-start | bytes 7077888 | tf_op jit(solution)/shard_map/all_gather | solution.py:65
  337.0 90.3 %copy-start.11 = (f32[2,64,3072]{2,1,0:T(8,128)S(1)}, f32[2,64,3072]{2,1,0:T(8,128)}, u32[]{:S(2)}) copy-start(f32[2,64,3072]{2,1,0:T(8,128)} %param.19) | copy-start | bytes 4718596
  337.0 90.3 %copy-start.12 = (f32[2,64,3072]{2,1,0:T(8,128)S(1)}, f32[2,64,3072]{2,1,0:T(8,128)}, u32[]{:S(2)}) copy-start(f32[2,64,3072]{2,1,0:T(8,128)} %param.16) | copy-start | bytes 4718596
  342.0 302.7 %all-gather.4.cloned.1.call-start = ((), (), s32[]{:S(2)}) async-start(), calls=%async_computation.8 | async-start | bytes 7077888 | tf_op jit(solution)/shard_map/all_gather | solution.py:65
  644.6 6.6 copy-start.3
  644.6 9.8 %slice-start = ((s8[6291456]{0:T(1024)(128)(4,1)}), s8[4194304]{0:T(1024)(128)(4,1)S(1)}, s32[]{:S(2)}) async-start(s8[6291456]{0:T(1024)(128)(4,1)} %bitcast.76), calls=%async_computation.15 | async-start | bytes 8388608
  651.3 4.5 slice-start.1
Sparse Core Ops, SparseCore 0:
  156.7 45.5 reduce-scatter.14
  204.7 42.3 reduce-scatter.16
  249.5 42.3 reduce-scatter.10
  294.7 42.2 reduce-scatter.12
  339.8 42.3 reduce-scatter.6
  385.0 42.3 reduce-scatter.8
  428.9 72.0 all-gather.7
  503.2 69.5 all-gather.5
  575.0 69.5 all-gather.3

commit v2 on v0

v2 whole, which is shorter than its diff:
```python
import functools

import jax
import jax.numpy as jnp
from jax import lax
from jax.experimental import pallas as pl
from jax.experimental.pallas import tpu as pltpu
from jax.sharding import PartitionSpec as P

F32 = jnp.float32
BF16 = jnp.bfloat16
MESH = pl.DeviceIdType.MESH
STRIP = 128
WIDE = 2 * STRIP
SLOTS = 6
AG_FROM = 8
COMM = True
COMPUTE = True


def dot(a, b, dims=((1,), (0,))):
    return lax.dot_general(a, b, (dims, ((), ())), preferred_element_type=F32)


def aligned(i, m):
    return pl.multiple_of(i, m)


def kernel(
    n, x, dy, wg, wu, wd, mg, mu, md, vg, vu, vd,
    og, ou, od, omg, omu, omd, ovg, ovu, ovd,
    h_ref, a_ref, at_ref, ct_ref, acc_ref, p_ref, dgu_ref, wgu_buf, wd_buf,
    g_gu, g_dn, land_gu, land_dn, m_gu, v_gu, m_dn, v_dn, own_gu, own_dn,
    w_sem, in_sem, out_sem, gu_send, gu_recv, dn_send, dn_recv, ag_send, ag_recv,
):
    tokens, d = h_ref.shape
    layers, _, ff = wg.shape
    rows = d // n
    share = ff // n
    per_layer = ff // WIDE
    per_chunk = n // 2
    chunks = per_layer // per_chunk
    tiles = layers * per_layer
    half = STRIP // 2
    block = tokens // 4
    me, rep = lax.axis_index("dp"), lax.axis_index("rep")
    right, left = lax.rem(me + 1, n), lax.rem(me + n - 1, n)
    to = (right, left)

    def owner(direction, hop):
        return lax.rem(me + n - 1 - hop, n) if direction == 0 else lax.rem(me + 1 + hop, n)

    def holder(direction, hop):
        return lax.rem(me + n - hop, n) if direction == 0 else lax.rem(me + hop, n)

    def place(t):
        tt = lax.rem(t, per_layer)
        return layers - 1 - lax.div(t, per_layer), lax.div(tt, per_chunk), lax.rem(tt, per_chunk)

    def strips(j, i):
        return [aligned((2 * i + k) * share + STRIP * j, STRIP) for k in range(2)]

    def tile_copies(g):
        lay = lax.rem(lax.div(g, per_layer), 2)
        tt = lax.rem(g, per_layer)
        cols = strips(lax.div(tt, per_chunk), lax.rem(tt, per_chunk))
        slot = lax.rem(g, 2)
        out = []
        for k, col in enumerate(cols):
            strip = pl.ds(col, STRIP)
            for q, w in enumerate((wg, wu)):
                out.append((w.at[lay, :, strip], wgu_buf.at[slot, :, pl.ds(q * WIDE + k * STRIP, STRIP)]))
            out.append((wd.at[lay, strip], wd_buf.at[slot, pl.ds(k * STRIP, STRIP)]))
        return [pltpu.make_async_copy(a, b, w_sem.at[slot, k]) for k, (a, b) in enumerate(out)]

    def fetch(g):
        for c in tile_copies(g):
            c.start()

    def fetched(g):
        for c in tile_copies(g):
            c.wait()

    load_x = pltpu.make_async_copy(x.at[0], h_ref, in_sem.at[0])
    load_dy = pltpu.make_async_copy(dy.at[0], ct_ref, in_sem.at[1])
    moments = [
        pltpu.make_async_copy(a, b, in_sem.at[2 + k])
        for k, (a, b) in enumerate(
            ((mg, m_gu.at[0]), (mu, m_gu.at[1]), (vg, v_gu.at[0]), (vu, v_gu.at[1]), (md, m_dn), (vd, v_dn),
             (wg.at[:, pl.ds(aligned(me * rows, rows), rows)], own_gu.at[0]),
             (wu.at[:, pl.ds(aligned(me * rows, rows), rows)], own_gu.at[1]),
             (wd.at[:, pl.ds(aligned(me * share, share), share)], own_dn))
        )
    ]

    def results(lay):
        mine, down = pl.ds(aligned(me * rows, rows), rows), pl.ds(aligned(me * share, share), share)
        pairs = (
            (m_gu.at[0, lay], omg.at[lay]), (m_gu.at[1, lay], omu.at[lay]), (m_dn.at[lay], omd.at[lay]),
            (v_gu.at[0, lay], ovg.at[lay]), (v_gu.at[1, lay], ovu.at[lay]), (v_dn.at[lay], ovd.at[lay]),
            (own_gu.at[0, lay], og.at[lay, mine]), (own_gu.at[1, lay], ou.at[lay, mine]), (own_dn.at[lay], od.at[lay, down]),
        )
        return [pltpu.make_async_copy(a, b, out_sem.at[lay, k]) for k, (a, b) in enumerate(pairs)]

    barrier = pltpu.get_barrier_semaphore()
    for other in to:
        pl.semaphore_signal(barrier, inc=1, device_id=(rep, other), device_id_type=MESH)
    load_x.start()
    fetch(0)
    load_dy.start()
    for c in moments:
        c.start()
    pl.semaphore_wait(barrier, 2)

    def remote(src, dst, send, recv, direction):
        return pltpu.make_async_remote_copy(
            src_ref=src, dst_ref=dst, send_sem=send, recv_sem=recv, device_id=(rep, to[direction]), device_id_type=MESH
        )

    def adam(w, m, v, g):
        g = g.astype(F32)
        m = 0.9 * m + 0.1 * g
        v = 0.95 * v + 0.05 * g * g
        step = m * lax.rsqrt(v + 1e-8) + 0.1 * w
        return (w - 0.02 * step).astype(BF16), m, v

    def gu_copy(u, s, direction):
        slot = lax.rem(u, SLOTS)
        if s == 0:
            src = g_gu.at[slot, direction, pl.ds(aligned(owner(direction, 0) * rows, rows), rows)]
        else:
            src = land_gu.at[slot, s - 1, direction]
        return remote(src, land_gu.at[slot, s, direction], gu_send.at[slot, direction], gu_recv.at[slot, s, direction], direction)

    def gu_event(u, s):
        slot = lax.rem(u, SLOTS)
        if s > 0:
            for e in range(2):
                before = gu_copy(u, s - 1, e)
                before.wait_send()
                before.wait_recv()
                mine = g_gu[slot, e, pl.ds(aligned(owner(e, s) * rows, rows), rows)]
                total = (land_gu[slot, s - 1, e].astype(F32) + mine.astype(F32)).astype(BF16)
                if s < n - 1:
                    land_gu[slot, s - 1, e] = total
                else:
                    lay, j, i = place(u)
                    for k, col in enumerate(strips(j, i)):
                        strip = pl.ds(col, STRIP)
                        new, m, v = adam(
                            own_gu[e, lay, :, strip].astype(F32), m_gu[e, lay, :, strip], v_gu[e, lay, :, strip],
                            total[:, k * STRIP : (k + 1) * STRIP],
                        )
                        own_gu[e, lay, :, strip] = new
                        m_gu[e, lay, :, strip] = m
                        v_gu[e, lay, :, strip] = v
        if s < n - 1:
            for e in range(2):
                gu_copy(u, s, e).start()

    def dn_first(c, e):
        slot = lax.rem(c, 2)
        src = g_dn.at[slot, owner(e, 0), pl.ds(e * half, half)]
        return remote(src, land_dn.at[slot, 0, e], dn_send.at[slot, e], dn_recv.at[slot, 0, e], e)

    def dn_next(c, s, e):
        slot = lax.rem(c, 2)
        return remote(land_dn.at[slot, s - 1, e], land_dn.at[slot, s, e], dn_send.at[slot, e], dn_recv.at[slot, s, e], e)

    def dn_event(c, s):
        slot = lax.rem(c, 2)

        @pl.when(s == 0)
        def _():
            for e in range(2):
                dn_first(c, e).start()

        @pl.when(s > 0)
        def _():
            for e in range(2):
                before = remote(
                    land_dn.at[slot, s - 1, e], land_dn.at[slot, s - 1, e], dn_send.at[slot, e], dn_recv.at[slot, s - 1, e], e
                )
                before.wait_send()
                before.wait_recv()
                mine = g_dn[slot, owner(e, s), pl.ds(e * half, half)]
                land_dn[slot, s - 1, e] = (land_dn[slot, s - 1, e].astype(F32) + mine.astype(F32)).astype(BF16)

            @pl.when(s < n - 1)
            def _():
                for e in range(2):
                    dn_next(c, s, e).start()

            @pl.when(s == n - 1)
            def _():
                lay, j, _ = place(c * per_chunk)
                for e in range(2):
                    r = pl.ds(aligned(STRIP * j + e * half, half), half)
                    new, m, v = adam(own_dn[lay, r].astype(F32), m_dn[lay, r], v_dn[lay, r], land_dn[slot, n - 2, e])
                    own_dn[lay, r] = new
                    m_dn[lay, r] = m
                    v_dn[lay, r] = v

    def ag_start(c, h, first):
        lay, j, _ = place(c * per_chunk)
        for e in range(2):
            who = holder(e, h)
            r = pl.ds(aligned(who * rows, rows), rows)
            out = (og, ou)[e]
            send, recv = ag_send.at[c, e], ag_recv.at[c, h, e]

            def strip_copy(i, _):
                strip = pl.ds(aligned(i * share + STRIP * j, STRIP), STRIP)
                there = out.at[lay, r, strip]
                remote(own_gu.at[e, lay, :, strip] if first else there, there, send, recv, e).start()
                return 0

            lax.fori_loop(0, n, strip_copy, 0)
            there = od.at[lay, pl.ds(aligned(who * share + STRIP * j + e * half, half), half)]
            src = own_dn.at[lay, pl.ds(aligned(STRIP * j + e * half, half), half)] if first else there
            remote(src, there, send, recv, e).start()

    def ag_wait(c, h):
        sent = (n * rows * STRIP + half * d) // d
        for e in range(2):
            all_of_it = od.at[0, pl.ds(0, sent)]
            before = remote(all_of_it, all_of_it, ag_send.at[c, e], ag_recv.at[c, h, e], e)
            before.wait_send()
            before.wait_recv()

    def ag_event(c, h):
        @pl.when(h == 0)
        def _():
            ag_start(c, 0, True)

        @pl.when(h > 0)
        def _():
            ag_wait(c, h - 1)

            @pl.when(h < n - 1)
            def _():
                ag_start(c, h, False)

    def pump(t, part):
        if not COMM:
            return
        for back in range(1, per_chunk + 1):
            s = 2 * (back - 1) + part
            if s > n - 1:
                continue

            @pl.when((t >= back) & (t - back < tiles))
            def _():
                gu_event(t - back, s)

        @pl.when(t >= per_chunk)
        def _():
            dn_event(lax.div(t, per_chunk) - 1, 2 * lax.rem(t, per_chunk) + part)

        if part == 1:

            @pl.when(t >= AG_FROM)
            def _():
                ag_event(lax.div(t - AG_FROM, n), lax.rem(t - AG_FROM, n))

            @pl.when(t == 4 * per_chunk)
            def _():
                for c in results(layers - 1):
                    c.start()

    def normalise(b, _):
        r = pl.ds(aligned(b * 256, 256), 256)
        wide = h_ref[r].astype(F32)
        scale = lax.rsqrt(jnp.mean(wide * wide, -1, keepdims=True) + 1e-6)
        a = wide * scale
        a_ref[r] = a.astype(BF16)
        at_ref[:, r] = a.T.astype(BF16)
        return 0

    def gates(r, slot):
        gu = dot(a_ref[r], wgu_buf[slot])
        gate, up = gu[:, :WIDE], gu[:, WIDE:]
        sig = jax.nn.sigmoid(gate)
        return gate * sig, up, sig

    load_x.wait()
    lax.fori_loop(0, tokens // 256, normalise, 0)
    acc_ref[...] = jnp.zeros_like(acc_ref)

    def forward(g, _):
        slot = lax.rem(g, 2)
        fetch(g + 1)
        fetched(g)
        for b in range(4):
            r = pl.ds(b * block, block)
            silu, up, _ = gates(r, slot)
            acc_ref[r] += dot((silu * up).astype(BF16), wd_buf[slot])
        return 0

    if COMPUTE:
        lax.fori_loop(0, per_layer, forward, 0)

    def join(b, _):
        r = pl.ds(aligned(b * 256, 256), 256)
        h_ref[r] = h_ref[r] + acc_ref[r].astype(BF16)
        acc_ref[r] = jnp.zeros((256, d), F32)
        return normalise(b, 0)

    lax.fori_loop(0, tokens // 256, join, 0)
    load_dy.wait()
    for c in moments:
        c.wait()

    def backward(t, _, with_da, last):
        g = t + per_layer
        slot = lax.rem(g, 2)
        if COMPUTE:
            if last:

                @pl.when(t < tiles - 1)
                def _():
                    fetch(g + 1)
            else:
                fetch(g + 1)
            fetched(g)
        lay, j, i = place(t)
        for b in range(4 if COMPUTE else 0):
            r = pl.ds(b * block, block)
            silu, up, sig = gates(r, slot)
            dp = dot(ct_ref[r], wd_buf[slot], ((1,), (1,))).astype(BF16).astype(F32)
            p_ref[r] = (silu * up).astype(BF16)
            dgu_ref[r, WIDE:] = (dp * silu).astype(BF16)
            dgu_ref[r, :WIDE] = (dp * up * (sig + silu * (1 - sig))).astype(BF16)
            if with_da:
                acc_ref[r] += dot(dgu_ref[r], wgu_buf[slot], ((1,), (1,)))
            if b == 0:
                pump(t, 0)
        if not COMPUTE:
            pump(t, 0)
        if COMPUTE:
            grads = dot(p_ref[...], ct_ref[...], ((0,), (0,))).astype(BF16)
            dslot = lax.rem(lax.div(t, per_chunk), 2)
            for k in range(2):
                g_dn[dslot, 2 * i + k] = grads[k * STRIP : (k + 1) * STRIP]
        pump(t, 1)
        if COMPUTE:
            grads = dot(at_ref[...], dgu_ref[...]).astype(BF16)
            for e in range(2):
                g_gu[lax.rem(t, SLOTS), e] = grads[:, e * WIDE : (e + 1) * WIDE]
        return 0

    lax.fori_loop(0, per_layer, functools.partial(backward, with_da=True, last=False), 0)

    def turn(b, _):
        r = pl.ds(aligned(b * 256, 256), 256)
        wide = h_ref[r].astype(F32)
        scale = lax.rsqrt(jnp.mean(wide * wide, -1, keepdims=True) + 1e-6)
        da = acc_ref[r].astype(BF16).astype(F32)
        inner = jnp.mean(da * wide, -1, keepdims=True)
        ct_ref[r] = ct_ref[r] + (da * scale - wide * (scale * scale * scale * inner)).astype(BF16)
        return 0

    lax.fori_loop(0, tokens // 256, turn, 0)
    load_x.start()
    load_x.wait()
    lax.fori_loop(0, tokens // 256, normalise, 0)
    lax.fori_loop(per_layer, tiles, functools.partial(backward, with_da=False, last=True), 0)

    def drain(t, _):
        pump(t, 0)
        pump(t, 1)
        return 0

    lax.fori_loop(tiles, tiles + per_chunk, drain, 0)
    for c in results(0):
        c.start()
    if COMM:
        done = tiles + per_chunk - AG_FROM
        part, begun = done % n, done // n

        def rest(h, _):
            for c in range(begun + (part > 0), layers * chunks):
                ag_event(c, h)
            if part:

                @pl.when(h + part < n)
                def _():
                    ag_event(begun, h + part)

            return 0

        lax.fori_loop(0, n, rest, 0)
    else:
        for c in results(layers - 1):
            c.start()
    for lay in range(layers):
        for c in results(lay):
            c.wait()


def device_step(n, x, dy, *arrays):
    w, m, v = (arrays[i : i + 3] for i in (0, 3, 6))
    layers, d, ff = w[0].shape
    tokens = x.shape[1]
    rows, share = d // n, ff // n
    hops, chunks = n - 1, share // STRIP * layers
    anywhere = pl.BlockSpec(memory_space=pl.ANY)
    dma = pltpu.SemaphoreType.DMA
    return pl.pallas_call(
        functools.partial(kernel, n),
        name="step",
        out_shape=[jax.ShapeDtypeStruct(a.shape, a.dtype) for a in (*w, *m, *v)],
        in_specs=[anywhere] * 11,
        out_specs=[anywhere] * 9,
        scratch_shapes=[
            pltpu.VMEM((tokens, d), BF16),
            pltpu.VMEM((tokens, d), BF16),
            pltpu.VMEM((d, tokens), BF16),
            pltpu.VMEM((tokens, d), BF16),
            pltpu.VMEM((tokens, d), F32),
            pltpu.VMEM((tokens, WIDE), BF16),
            pltpu.VMEM((tokens, 2 * WIDE), BF16),
            pltpu.VMEM((2, d, 2 * WIDE), BF16),
            pltpu.VMEM((2, WIDE, d), BF16),
            pltpu.VMEM((SLOTS, 2, d, WIDE), BF16),
            pltpu.VMEM((2, n, STRIP, d), BF16),
            pltpu.VMEM((SLOTS, hops, 2, rows, WIDE), BF16),
            pltpu.VMEM((2, hops, 2, STRIP // 2, d), BF16),
            pltpu.VMEM((2, layers, rows, ff), F32),
            pltpu.VMEM((2, layers, rows, ff), F32),
            pltpu.VMEM((layers, share, d), F32),
            pltpu.VMEM((layers, share, d), F32),
            pltpu.VMEM((2, layers, rows, ff), BF16),
            pltpu.VMEM((layers, share, d), BF16),
            dma((2, 6)),
            dma((11,)),
            dma((layers, 9)),
            dma((SLOTS, 2)),
            dma((SLOTS, hops, 2)),
            dma((2, 2)),
            dma((2, hops, 2)),
            dma((chunks, 2)),
            dma((chunks, hops, 2)),
        ],
        compiler_params=pltpu.CompilerParams(collective_id=0, has_side_effects=True, vmem_limit_bytes=63 * 2**20),
    )(x, dy, *arrays)


def solution(mesh):
    whole, rows, seq = P(None, None, None), P(None, "dp", None), P(("rep", "dp"), None, None)
    return jax.shard_map(
        functools.partial(device_step, mesh.shape["dp"]),
        mesh=mesh,
        in_specs=(seq, seq) + (whole,) * 3 + (rows,) * 6,
        out_specs=(P("rep", None, None),) * 3 + (P("rep", "dp", None),) * 6,
        check_vma=False,
    )
```

time: 873 us -> 455 us (0.52)
  the two profiles are of different devices: /device:TPU:21 before, /device:TPU:30 now
where the time goes in v2:
time: 455 us
  Pallas kernels  430 us (95%)
  local copies, waits for them, and re-layouts  24.8 us (5%)
    pallas_call x1, Pallas kernels, device_step(): pl.pallas_call(functools.partial(kernel, n), name='step', out_shape=[jax....  430 us
    unnamed x27, local copies, waits for them, and re-layouts  24.8 us

profile of v2, /device:TPU:30, one launch (start us, length us, event | category | flops | bytes accessed | tf_op | source)
XLA Modules:
  0.0 455.1 jit_solution(16578276949502551261)
XLA Ops:
  0.6 429.6 %step.1 = (bf16[2,512,3072]{2,1,0:T(8,128)(2,1)}, bf16[2,512,3072]{2,1,0:T(8,128)(2,1)}, bf16[2,3072,512]{2,1,0:T(8,128)(2,1)}, f32[2,64,3072]{2,1,0:T(8,128)}, ...) custom-call(bf16[1,2048,512]{2,1,0:T(8,128)(2,1)} %x.1, ...), custom_call_target="tpu_custom_call" | custom-call | tf_op jit(solution)/shard_map/step/pallas_call | solution.py:409
  430.3 0.0 copy-start
  430.3 0.0 slice-start
  430.3 6.6 %copy.29 = bf16[2,512,3072]{2,1,0:T(8,128)(2,1)} copy(bf16[2,512,3072]{2,1,0:T(8,128)(2,1)} %get-tuple-element.18) | data formatting | bytes 12582912
  436.9 0.0 copy-done
  436.9 0.0 slice-start.1
  436.9 3.2 copy.30
  440.1 0.0 slice-done
  440.1 1.3 slice-done.1
  441.4 0.0 copy-start.6
  441.4 2.7 copy.31
  444.1 0.0 copy-done.6
  444.1 0.0 copy-start.5
  444.1 1.1 copy.32
  445.2 0.8 copy-done.5
  446.1 0.0 copy-start.4
  446.1 1.1 copy.33
  447.2 0.8 copy-done.4
  448.1 0.0 copy-start.3
  448.1 1.1 copy.34
  449.2 0.8 copy-done.3
  450.0 0.0 copy-start.2
  450.0 1.1 copy.35
  451.2 0.8 copy-done.2
  452.0 0.0 copy-start.1
  452.0 1.1 copy.36
  453.1 0.8 copy-done.1
  454.0 1.1 copy.37
  (1 shorter events, 0.0 us)
Async XLA Ops:
  430.3 6.6 %copy-start = (bf16[2,512,3072]{2,1,0:T(8,128)(2,1)S(1)}, bf16[2,512,3072]{2,1,0:T(8,128)(2,1)}, u32[]{:S(2)}) copy-start(bf16[2,512,3072]{2,1,0:T(8,128)(2,1)} %get-tuple-element.19) | copy-start | bytes 18874372
  430.3 9.8 %slice-start = ((s8[6291456]{0:T(1024)(128)(4,1)}), s8[4194304]{0:T(1024)(128)(4,1)S(1)}, s32[]{:S(2)}) async-start(s8[6291456]{0:T(1024)(128)(4,1)} %bitcast), calls=%async_computation | async-start | bytes 8388608
  436.9 4.5 slice-start.1
  441.4 2.7 copy-start.6
  444.1 2.0 copy-start.5
  446.1 2.0 copy-start.4
  448.1 2.0 copy-start.3
  450.0 2.0 copy-start.2
  452.0 2.0 copy-start.1

commit v3 on v2

v3 whole, which is shorter than its diff:
```python
import functools

import jax
import jax.numpy as jnp
from jax import lax
from jax.experimental import pallas as pl
from jax.experimental.pallas import tpu as pltpu
from jax.sharding import PartitionSpec as P

F32 = jnp.float32
BF16 = jnp.bfloat16
MESH = pl.DeviceIdType.MESH
STRIP = 128
WIDE = 2 * STRIP
SLOTS = 6
DN_SLOTS = 3
DRAIN_UNITS = 4
LAG = 4
GROUPS = ((0, 1, 2, 3), (4, 5), (6, 7, 8, 9, 10))
STEPS = len(GROUPS)
GU_FROM = 2
DN_FROM = 3


def dot(a, b, dims=((1,), (0,))):
    return lax.dot_general(a, b, (dims, ((), ())), preferred_element_type=F32)


def aligned(i, m):
    return pl.multiple_of(i, m)


def kernel(
    n, x, dy, wg, wu, wd, mg, mu, md, vg, vu, vd,
    og, ou, od, omg, omu, omd, ovg, ovu, ovd,
    h_ref, a_ref, at_ref, ct_ref, acc_ref, p_ref, dgu_ref, wgu_buf, wd_buf,
    g_gu, g_dn, land_gu, land_dn,
    w_sem, in_sem, gu_send, gu_recv, dn_send, dn_recv, ag_send, ag_recv,
):
    tokens, d = h_ref.shape
    layers, _, ff = wg.shape
    rows = d // n
    share = ff // n
    per_layer = ff // WIDE
    per_chunk = n // 2
    chunks = layers * per_layer // per_chunk
    tiles = layers * per_layer
    half = STRIP // 2
    block = tokens // 4
    me, rep = lax.axis_index("dp"), lax.axis_index("rep")
    right, left = lax.rem(me + 1, n), lax.rem(me + n - 1, n)
    to = (right, left)

    longer = n // 2

    def length(e, direction):
        return longer if e == direction else n - 1 - longer

    def owner(e, direction, hop):
        away = length(e, direction) - hop
        return lax.rem(me + away, n) if direction == 0 else lax.rem(me + n - away, n)

    def holder(direction, hop):
        return lax.rem(me + n - hop, n) if direction == 0 else lax.rem(me + hop, n)

    def place(t):
        tt = lax.rem(t, per_layer)
        return layers - 1 - lax.div(t, per_layer), lax.div(tt, per_chunk), lax.rem(tt, per_chunk)

    def strips(j, i):
        return [aligned((2 * i + k) * share + STRIP * j, STRIP) for k in range(2)]

    def tile_copies(g):
        lay = lax.rem(lax.div(g, per_layer), 2)
        tt = lax.rem(g, per_layer)
        cols = strips(lax.div(tt, per_chunk), lax.rem(tt, per_chunk))
        slot = lax.rem(g, 2)
        out = []
        for k, col in enumerate(cols):
            strip = pl.ds(col, STRIP)
            for q, w in enumerate((wg, wu)):
                out.append((w.at[lay, :, strip], wgu_buf.at[slot, :, pl.ds(q * WIDE + k * STRIP, STRIP)]))
            out.append((wd.at[lay, strip], wd_buf.at[slot, pl.ds(k * STRIP, STRIP)]))
        return [pltpu.make_async_copy(a, b, w_sem.at[slot, k]) for k, (a, b) in enumerate(out)]

    def fetch(g):
        for c in tile_copies(g):
            c.start()

    def fetched(g):
        for c in tile_copies(g):
            c.wait()

    load_x = pltpu.make_async_copy(x.at[0], h_ref, in_sem.at[0])
    load_dy = pltpu.make_async_copy(dy.at[0], ct_ref, in_sem.at[1])
    my_rows, my_share = pl.ds(aligned(me * rows, rows), rows), pl.ds(aligned(me * share, share), share)
    moments = [
        pltpu.make_async_copy(a, b, in_sem.at[2 + k])
        for k, (a, b) in enumerate(
            ((mg, omg), (mu, omu), (md, omd), (vg, ovg), (vu, ovu), (vd, ovd),
             (wg.at[:, my_rows], og.at[:, my_rows]), (wu.at[:, my_rows], ou.at[:, my_rows]), (wd.at[:, my_share], od.at[:, my_share]))
        )
    ]

    barrier = pltpu.get_barrier_semaphore()
    for other in to:
        pl.semaphore_signal(barrier, inc=1, device_id=(rep, other), device_id_type=MESH)
    load_x.start()
    fetch(0)
    load_dy.start()

    def remote(src, dst, send, recv, direction):
        return pltpu.make_async_remote_copy(
            src_ref=src, dst_ref=dst, send_sem=send, recv_sem=recv, device_id=(rep, to[direction]), device_id_type=MESH
        )

    def adam(w, m, v, g):
        g = g.astype(F32)
        m = 0.9 * m + 0.1 * g
        v = 0.95 * v + 0.05 * g * g
        step = m * lax.rsqrt(v + 1e-8) + 0.1 * w
        return (w - 0.02 * step).astype(BF16), m, v

    def sum_event(hop, own, land, send, recv, update):
        def copy(e, direction, h):
            src = own(e, owner(e, direction, 0)) if h == 0 else land.at[e, direction, h - 1]
            return remote(src, land.at[e, direction, h], send.at[e, direction], recv.at[e, direction, h], direction)

        def ended(e, direction, h):
            before = copy(e, direction, h)
            before.wait_send()
            before.wait_recv()
            return land[e, direction, h].astype(F32)

        if hop == longer:
            for e in range(2):
                whole = own(e, me)[...].astype(F32)
                for direction in range(2):
                    whole += ended(e, direction, length(e, direction) - 1)
                update(e, whole.astype(BF16))
            return
        ready = []
        for e, direction in ((0, 0), (1, 1), (1, 0), (0, 1)):
            if hop >= length(e, direction):
                continue
            if hop > 0:
                mine = own(e, owner(e, direction, hop))[...].astype(F32)
                land[e, direction, hop - 1] = (ended(e, direction, hop - 1) + mine).astype(BF16)
            ready.append(copy(e, direction, hop))
            if len(ready) > 1:
                ready[-2].start()
        ready[-1].start()

    def gu_event(u, hop):
        slot = lax.rem(u, SLOTS)
        lay, j, i = place(u)

        def update(e, g):
            w, m, v = ((og, omg, ovg), (ou, omu, ovu))[e]
            for k, col in enumerate(strips(j, i)):
                strip = pl.ds(col, STRIP)
                w[lay, my_rows, strip], m[lay, :, strip], v[lay, :, strip] = adam(
                    w[lay, my_rows, strip].astype(F32), m[lay, :, strip], v[lay, :, strip], g[:, k * STRIP : (k + 1) * STRIP]
                )

        def own(e, who):
            return g_gu.at[slot, e, pl.ds(aligned(who * rows, rows), rows)]

        sum_event(hop, own, land_gu.at[slot], gu_send.at[slot], gu_recv.at[slot], update)

    def dn_event(c, hop):
        slot = lax.rem(c, DN_SLOTS)
        lay, j, _ = place(c * per_chunk)

        def update(e, g):
            r = pl.ds(aligned(STRIP * j + e * half, half), half)
            mine = pl.ds(aligned(me * share + STRIP * j + e * half, half), half)
            od[lay, mine], omd[lay, r], ovd[lay, r] = adam(od[lay, mine].astype(F32), omd[lay, r], ovd[lay, r], g)

        def own(e, who):
            return g_dn.at[slot, who, pl.ds(e * half, half)]

        sum_event(hop, own, land_dn.at[slot], dn_send.at[slot], dn_recv.at[slot], update)

    def new_copies(c, e, direction, h):
        lay, j, _ = place(c * per_chunk)
        who = holder(direction, h)
        send, recv = ag_send.at[c, e, direction], ag_recv.at[c, e, direction, h]
        out, r = (og, ou)[e], pl.ds(aligned(who * rows, rows), rows)

        for i in range(n):
            there = out.at[lay, r, pl.ds(aligned(i * share + STRIP * j, STRIP), STRIP)]
            remote(there, there, send, recv, direction).start()
        there = od.at[lay, pl.ds(aligned(who * share + STRIP * j + e * half, half), half)]
        remote(there, there, send, recv, direction).start()

    def new_ended(c, e, direction, h):
        sent = (n * rows * STRIP + half * d) // d
        all_of_it = od.at[0, pl.ds(0, sent)]
        before = remote(all_of_it, all_of_it, ag_send.at[c, e, direction], ag_recv.at[c, e, direction, h], direction)
        before.wait_send()
        before.wait_recv()

    def ag_event(unit, hop):
        c = lax.div(unit, 2)
        for e in range(2):

            @pl.when(lax.rem(unit, 2) == e)
            def _():
                for direction in range(2):

                    @pl.when((hop > 0) & (hop < length(e, direction)))
                    def _():
                        new_ended(c, e, direction, hop - 1)

                for direction in range(2):

                    @pl.when(hop < length(e, direction))
                    def _():
                        new_copies(c, e, direction, hop)

    def pump(t, step):
        for hop in range(longer + 1):
            since, due = divmod(GU_FROM + LAG * hop, STEPS)
            if due == step:

                @pl.when((t >= since) & (t < tiles + since))
                def _():
                    gu_event(t - since, hop)

            since, due = divmod(DN_FROM + LAG * hop, STEPS)
            if due == step:

                @pl.when((t >= since) & (t < tiles + since) & (lax.rem(t - since + 1, per_chunk) == 0))
                def _():
                    dn_event(lax.div(t - since, per_chunk), hop)

    def normalise(b, _, turned=True):
        r = pl.ds(aligned(b * 256, 256), 256)
        wide = h_ref[r].astype(F32)
        scale = lax.rsqrt(jnp.mean(wide * wide, -1, keepdims=True) + 1e-6)
        a = wide * scale
        a_ref[r] = a.astype(BF16)
        if turned:
            at_ref[:, r] = a.T.astype(BF16)
        return 0

    def gates(r, slot):
        gu = dot(a_ref[r], wgu_buf[slot])
        gate, up = gu[:, :WIDE], gu[:, WIDE:]
        sig = jax.nn.sigmoid(gate)
        return gate * sig, up, sig

    load_x.wait()
    lax.fori_loop(0, tokens // 256, functools.partial(normalise, turned=False), 0)
    acc_ref[...] = jnp.zeros_like(acc_ref)

    def forward(g, _):
        slot = lax.rem(g, 2)
        fetch(g + 1)
        fetched(g)
        for b in range(4):
            r = pl.ds(b * block, block)
            silu, up, _ = gates(r, slot)
            acc_ref[r] += dot((silu * up).astype(BF16), wd_buf[slot])
        return 0

    lax.fori_loop(0, per_layer, forward, 0)

    def join(b, _):
        r = pl.ds(aligned(b * 256, 256), 256)
        h_ref[r] = h_ref[r] + acc_ref[r].astype(BF16)
        acc_ref[r] = jnp.zeros((256, d), F32)
        return normalise(b, 0)

    lax.fori_loop(0, tokens // 256, join, 0)
    load_dy.wait()
    pl.semaphore_wait(barrier, 2)
    for c in moments:
        c.start()

    def backward(t, _, with_da, last):
        g = t + per_layer
        slot = lax.rem(g, 2)
        if last:

            @pl.when(t < tiles - 1)
            def _():
                fetch(g + 1)
        else:
            fetch(g + 1)
        fetched(g)
        lay, j, i = place(t)
        if with_da:

            @pl.when(t == 2)
            def _():
                for c in moments:
                    c.wait()

        def rows_of(b):
            r = pl.ds(b * block, block)
            silu, up, sig = gates(r, slot)
            dp = dot(ct_ref[r], wd_buf[slot], ((1,), (1,))).astype(BF16).astype(F32)
            p_ref[r] = (silu * up).astype(BF16)
            dgu_ref[r, WIDE:] = (dp * silu).astype(BF16)
            dgu_ref[r, :WIDE] = (dp * up * (sig + silu * (1 - sig))).astype(BF16)

        def da(b):
            if with_da:
                r = pl.ds(b * block, block)
                acc_ref[r] += dot(dgu_ref[r], wgu_buf[slot], ((1,), (1,)))

        def up_and_gate(e):
            g_gu[lax.rem(t, SLOTS), e] = dot(at_ref[...], dgu_ref[:, e * WIDE : (e + 1) * WIDE]).astype(BF16)

        def down():
            grads = dot(p_ref[...], ct_ref[...], ((0,), (0,))).astype(BF16)
            for k in range(2):
                g_dn[lax.rem(lax.div(t, per_chunk), DN_SLOTS), 2 * i + k] = grads[k * STRIP : (k + 1) * STRIP]

        work = [functools.partial(rows_of, b) for b in range(4)]
        work += [functools.partial(up_and_gate, 0), functools.partial(up_and_gate, 1), down]
        work += [functools.partial(da, b) for b in range(4)]
        for step in range(STEPS):
            pump(t, step)
            for k in GROUPS[step]:
                work[k]()
        return 0

    lax.fori_loop(0, per_layer, functools.partial(backward, with_da=True, last=False), 0)

    def turn(b, _):
        r = pl.ds(aligned(b * 256, 256), 256)
        wide = h_ref[r].astype(F32)
        scale = lax.rsqrt(jnp.mean(wide * wide, -1, keepdims=True) + 1e-6)
        da = acc_ref[r].astype(BF16).astype(F32)
        inner = jnp.mean(da * wide, -1, keepdims=True)
        ct_ref[r] = ct_ref[r] + (da * scale - wide * (scale * scale * scale * inner)).astype(BF16)
        return 0

    lax.fori_loop(0, tokens // 256, turn, 0)
    load_x.start()
    load_x.wait()
    lax.fori_loop(0, tokens // 256, normalise, 0)
    lax.fori_loop(per_layer, tiles, functools.partial(backward, with_da=False, last=True), 0)

    def drain(t, _):
        for step in range(STEPS):
            pump(t, step)
            event = STEPS * (t - tiles) + step

            @pl.when(event < DRAIN_UNITS * longer)
            def _():
                ag_event(lax.rem(event, DRAIN_UNITS), lax.div(event, DRAIN_UNITS))

        return 0

    drained = (STEPS * (tiles - 1) + DN_FROM + LAG * longer) // STEPS + 1
    lax.fori_loop(tiles, drained, drain, 0)

    def rest(event, _):
        units = 2 * chunks - DRAIN_UNITS
        ag_event(DRAIN_UNITS + lax.rem(event, units), lax.div(event, units))
        return 0

    lax.fori_loop(0, (2 * chunks - DRAIN_UNITS) * longer, rest, 0)

    def last(c, _):
        for e in range(2):
            for direction in range(2):
                new_ended(c, e, direction, length(e, direction) - 1)
        return 0

    lax.fori_loop(0, chunks, last, 0)


def put(*refs):
    *pairs, sem = refs
    copies = [pltpu.make_async_copy(a, b, sem.at[k]) for k, (a, b) in enumerate(zip(pairs[:9], pairs[9:]))]
    for c in copies:
        c.start()
    for c in copies:
        c.wait()


def device_step(n, x, dy, *arrays):
    w, m, v = (arrays[i : i + 3] for i in (0, 3, 6))
    layers, d, ff = w[0].shape
    tokens = x.shape[1]
    rows, share = d // n, ff // n
    hops, chunks = n // 2, share // STRIP * layers
    anywhere = pl.BlockSpec(memory_space=pl.ANY)
    dma = pltpu.SemaphoreType.DMA
    made = pl.pallas_call(
        functools.partial(kernel, n),
        name="step",
        out_shape=[pltpu.VMEM(a.shape, a.dtype) for a in (*w, *m, *v)],
        in_specs=[anywhere] * 11,
        out_specs=[pl.BlockSpec(memory_space=pltpu.VMEM)] * 9,
        scratch_shapes=[
            pltpu.VMEM((tokens, d), BF16),
            pltpu.VMEM((tokens, d), BF16),
            pltpu.VMEM((d, tokens), BF16),
            pltpu.VMEM((tokens, d), BF16),
            pltpu.VMEM((tokens, d), F32),
            pltpu.VMEM((tokens, WIDE), BF16),
            pltpu.VMEM((tokens, 2 * WIDE), BF16),
            pltpu.VMEM((2, d, 2 * WIDE), BF16),
            pltpu.VMEM((2, WIDE, d), BF16),
            pltpu.VMEM((SLOTS, 2, d, WIDE), BF16),
            pltpu.VMEM((DN_SLOTS, n, STRIP, d), BF16),
            pltpu.VMEM((SLOTS, 2, 2, hops, rows, WIDE), BF16),
            pltpu.VMEM((DN_SLOTS, 2, 2, hops, STRIP // 2, d), BF16),
            dma((2, 6)),
            dma((11,)),
            dma((SLOTS, 2, 2)),
            dma((SLOTS, 2, 2, hops)),
            dma((DN_SLOTS, 2, 2)),
            dma((DN_SLOTS, 2, 2, hops)),
            dma((chunks, 2, 2)),
            dma((chunks, 2, 2, hops)),
        ],
        compiler_params=pltpu.CompilerParams(collective_id=0, has_side_effects=True, vmem_limit_bytes=33 * 2**20),
    )(x, dy, *arrays)
    return pl.pallas_call(
        put,
        name="put",
        out_shape=[jax.ShapeDtypeStruct(a.shape, a.dtype) for a in made],
        in_specs=[pl.BlockSpec(memory_space=pltpu.VMEM)] * 9,
        out_specs=[anywhere] * 9,
        scratch_shapes=[dma((9,))],
        compiler_params=pltpu.CompilerParams(vmem_limit_bytes=2**20),
    )(*(pltpu.with_memory_space_constraint(a, pltpu.VMEM) for a in made))


def solution(mesh):
    whole, rows, seq = P(None, None, None), P(None, "dp", None), P(("rep", "dp"), None, None)
    return jax.shard_map(
        functools.partial(device_step, mesh.shape["dp"]),
        mesh=mesh,
        in_specs=(seq, seq) + (whole,) * 3 + (rows,) * 6,
        out_specs=(P("rep", None, None),) * 3 + (P("rep", "dp", None),) * 6,
        check_vma=False,
    )
```

time: 455 us -> 414 us (0.910)
  the two profiles are of different devices: /device:TPU:30 before, /device:TPU:21 now
where the time goes in v3:
time: 414 us
  Pallas kernels  413 us (100%)
    pallas_call x1, Pallas kernels, device_step(): pl.pallas_call(functools.partial(kernel, n), name='step', out_shape=[pltp...  404 us
    pallas_call x1, Pallas kernels, device_step(): pl.pallas_call(put, name='put', out_shape=[jax.ShapeDtypeStruct(a.shape,...  9.45 us

profile of v3, /device:TPU:21, one launch (start us, length us, event | category | flops | bytes accessed | tf_op | source)
XLA Modules:
  0.0 413.9 jit_solution(1410161781942274004)
XLA Ops:
  0.6 403.6 %step.1 = (bf16[2,512,3072]{2,1,0:T(8,128)(2,1)S(1)}, bf16[2,512,3072]{2,1,0:T(8,128)(2,1)S(1)}, bf16[2,3072,512]{2,1,0:T(8,128)(2,1)S(1)}, f32[2,64,3072]{2,1,0...) custom-call(bf16[1,2048,512]{2,1,0:T(8,128)(2,1)} %x.1, ...), custom_call_target="tpu_custom_call" | custom-call | tf_op jit(solution)/shard_map/step/pallas_call | solution.py:395
  404.2 9.4 %put.1 = (bf16[2,512,3072]{2,1,0:T(8,128)(2,1)}, bf16[2,512,3072]{2,1,0:T(8,128)(2,1)}, bf16[2,3072,512]{2,1,0:T(8,128)(2,1)}, f32[2,64,3072]{2,1,0:T(8,128)}, f...) custom-call(bf16[2,512,3072]{2,1,0:T(8,128)(2,1)S(1)} %get-tuple-ele, ...), custom_call_target="tpu_custom_call" | custom-call | tf_op jit(solution)/shard_map/put/pallas_call | solution.py:426

commit v4 on v3

--- a/solution.py
+++ b/solution.py
@@ -47,6 +47,7 @@
     tiles = layers * per_layer
     half = STRIP // 2
     block = tokens // 4
+    few = min(block, 256)
     me, rep = lax.axis_index("dp"), lax.axis_index("rep")
     right, left = lax.rem(me + 1, n), lax.rem(me + n - 1, n)
     to = (right, left)
@@ -74,7 +75,7 @@
         lay = lax.rem(lax.div(g, per_layer), 2)
         tt = lax.rem(g, per_layer)
         cols = strips(lax.div(tt, per_chunk), lax.rem(tt, per_chunk))
-        slot = lax.rem(g, 2)
+        slot = lax.rem(g, 4)
         out = []
         for k, col in enumerate(cols):
             strip = pl.ds(col, STRIP)
@@ -91,7 +92,8 @@
         for c in tile_copies(g):
             c.wait()
 
-    load_x = pltpu.make_async_copy(x.at[0], h_ref, in_sem.at[0])
+    parts = [pl.ds(b * block, block) for b in range(4)]
+    load_x = [pltpu.make_async_copy(x.at[0, r], h_ref.at[r], in_sem.at[11 + b]) for b, r in enumerate(parts)]
     load_dy = pltpu.make_async_copy(dy.at[0], ct_ref, in_sem.at[1])
     my_rows, my_share = pl.ds(aligned(me * rows, rows), rows), pl.ds(aligned(me * share, share), share)
     moments = [
@@ -105,8 +107,10 @@
     barrier = pltpu.get_barrier_semaphore()
     for other in to:
         pl.semaphore_signal(barrier, inc=1, device_id=(rep, other), device_id_type=MESH)
-    load_x.start()
+    for c in load_x:
+        c.start()
     fetch(0)
+    fetch(1)
     load_dy.start()
 
     def remote(src, dst, send, recv, direction):
@@ -169,7 +173,7 @@
         sum_event(hop, own, land_gu.at[slot], gu_send.at[slot], gu_recv.at[slot], update)
 
     def dn_event(c, hop):
-        slot = lax.rem(c, DN_SLOTS)
+        slot, there = lax.rem(c, DN_SLOTS), lax.rem(c, 2)
         lay, j, _ = place(c * per_chunk)
 
         def update(e, g):
@@ -180,7 +184,7 @@
         def own(e, who):
             return g_dn.at[slot, who, pl.ds(e * half, half)]
 
-        sum_event(hop, own, land_dn.at[slot], dn_send.at[slot], dn_recv.at[slot], update)
+        sum_event(hop, own, land_dn.at[there], dn_send.at[there], dn_recv.at[there], update)
 
     def new_copies(c, e, direction, h):
         lay, j, _ = place(c * per_chunk)
@@ -236,7 +240,7 @@
                     dn_event(lax.div(t - since, per_chunk), hop)
 
     def normalise(b, _, turned=True):
-        r = pl.ds(aligned(b * 256, 256), 256)
+        r = pl.ds(aligned(b * few, few), few)
         wide = h_ref[r].astype(F32)
         scale = lax.rsqrt(jnp.mean(wide * wide, -1, keepdims=True) + 1e-6)
         a = wide * scale
@@ -251,47 +255,55 @@
         sig = jax.nn.sigmoid(gate)
         return gate * sig, up, sig
 
-    load_x.wait()
-    lax.fori_loop(0, tokens // 256, functools.partial(normalise, turned=False), 0)
-    acc_ref[...] = jnp.zeros_like(acc_ref)
-
-    def forward(g, _):
-        slot = lax.rem(g, 2)
-        fetch(g + 1)
-        fetched(g)
+    def each(b, do):
+        for k in range(block // few):
+            do(b * (block // few) + k, 0)
+
+    def forward(pair, _, first=False):
+        g = 2 * pair
+        slot = lax.rem(g, 4)
+        for k in range(2):
+            fetch(g + 2 + k)
+            fetched(g + k)
         for b in range(4):
             r = pl.ds(b * block, block)
-            silu, up, _ = gates(r, slot)
-            acc_ref[r] += dot((silu * up).astype(BF16), wd_buf[slot])
-        return 0
-
-    lax.fori_loop(0, per_layer, forward, 0)
+            if first:
+                load_x[b].wait()
+                each(b, functools.partial(normalise, turned=False))
+            act = []
+            for k in range(2):
+                silu, up, _ = gates(r, slot + k)
+                act.append((silu * up).astype(BF16))
+            part = dot(jnp.concatenate(act, 1), wd_buf[pl.ds(slot, 2)].reshape(2 * WIDE, d))
+            acc_ref[r] = part if first else acc_ref[r] + part
+        return 0
+
+    forward(0, 0, first=True)
+    lax.fori_loop(1, per_layer // 2, forward, 0)
 
     def join(b, _):
-        r = pl.ds(aligned(b * 256, 256), 256)
+        r = pl.ds(aligned(b * few, few), few)
         h_ref[r] = h_ref[r] + acc_ref[r].astype(BF16)
-        acc_ref[r] = jnp.zeros((256, d), F32)
         return normalise(b, 0)
 
-    lax.fori_loop(0, tokens // 256, join, 0)
     load_dy.wait()
     pl.semaphore_wait(barrier, 2)
     for c in moments:
         c.start()
 
-    def backward(t, _, with_da, last):
+    def backward(t, _, with_da, last, first=False):
         g = t + per_layer
-        slot = lax.rem(g, 2)
+        slot = lax.rem(g, 4)
         if last:
 
-            @pl.when(t < tiles - 1)
+            @pl.when(t < tiles - 2)
             def _():
-                fetch(g + 1)
+                fetch(g + 2)
         else:
-            fetch(g + 1)
+            fetch(g + 2)
         fetched(g)
         lay, j, i = place(t)
-        if with_da:
+        if with_da and not first:
 
             @pl.when(t == 2)
             def _():
@@ -300,6 +312,8 @@
 
         def rows_of(b):
             r = pl.ds(b * block, block)
+            if first:
+                each(b, join)
             silu, up, sig = gates(r, slot)
             dp = dot(ct_ref[r], wd_buf[slot], ((1,), (1,))).astype(BF16).astype(F32)
             p_ref[r] = (silu * up).astype(BF16)
@@ -309,7 +323,8 @@
         def da(b):
             if with_da:
                 r = pl.ds(b * block, block)
-                acc_ref[r] += dot(dgu_ref[r], wgu_buf[slot], ((1,), (1,)))
+                part = dot(dgu_ref[r], wgu_buf[slot], ((1,), (1,)))
+                acc_ref[r] = part if first else acc_ref[r] + part
 
         def up_and_gate(e):
             g_gu[lax.rem(t, SLOTS), e] = dot(at_ref[...], dgu_ref[:, e * WIDE : (e + 1) * WIDE]).astype(BF16)
@@ -323,15 +338,19 @@
         work += [functools.partial(up_and_gate, 0), functools.partial(up_and_gate, 1), down]
         work += [functools.partial(da, b) for b in range(4)]
         for step in range(STEPS):
-            pump(t, step)
+            if not first:
+                pump(t, step)
+            elif step == GU_FROM:
+                gu_event(0, 0)
             for k in GROUPS[step]:
                 work[k]()
         return 0
 
-    lax.fori_loop(0, per_layer, functools.partial(backward, with_da=True, last=False), 0)
+    backward(0, 0, with_da=True, last=False, first=True)
+    lax.fori_loop(1, per_layer, functools.partial(backward, with_da=True, last=False), 0)
 
     def turn(b, _):
-        r = pl.ds(aligned(b * 256, 256), 256)
+        r = pl.ds(aligned(b * few, few), few)
         wide = h_ref[r].astype(F32)
         scale = lax.rsqrt(jnp.mean(wide * wide, -1, keepdims=True) + 1e-6)
         da = acc_ref[r].astype(BF16).astype(F32)
@@ -339,10 +358,12 @@
         ct_ref[r] = ct_ref[r] + (da * scale - wide * (scale * scale * scale * inner)).astype(BF16)
         return 0
 
-    lax.fori_loop(0, tokens // 256, turn, 0)
-    load_x.start()
-    load_x.wait()
-    lax.fori_loop(0, tokens // 256, normalise, 0)
+    lax.fori_loop(0, tokens // few, turn, 0)
+    for c in load_x:
+        c.start()
+    for c in load_x:
+        c.wait()
+    lax.fori_loop(0, tokens // few, normalise, 0)
     lax.fori_loop(per_layer, tiles, functools.partial(backward, with_da=False, last=True), 0)
 
     def drain(t, _):
@@ -358,7 +379,6 @@
 
     drained = (STEPS * (tiles - 1) + DN_FROM + LAG * longer) // STEPS + 1
     lax.fori_loop(tiles, drained, drain, 0)
-
     def rest(event, _):
         units = 2 * chunks - DRAIN_UNITS
         ag_event(DRAIN_UNITS + lax.rem(event, units), lax.div(event, units))
@@ -377,7 +397,10 @@
 
 def put(*refs):
     *pairs, sem = refs
-    copies = [pltpu.make_async_copy(a, b, sem.at[k]) for k, (a, b) in enumerate(zip(pairs[:9], pairs[9:]))]
+    copies = []
+    for k, (a, b) in enumerate(zip(pairs[:9], pairs[9:])):
+        for lay in range(a.shape[0]):
+            copies.append(pltpu.make_async_copy(a.at[lay], b.at[lay], sem.at[k, lay]))
     for c in copies:
         c.start()
     for c in copies:
@@ -406,22 +429,22 @@
             pltpu.VMEM((tokens, d), F32),
             pltpu.VMEM((tokens, WIDE), BF16),
             pltpu.VMEM((tokens, 2 * WIDE), BF16),
-            pltpu.VMEM((2, d, 2 * WIDE), BF16),
-            pltpu.VMEM((2, WIDE, d), BF16),
+            pltpu.VMEM((4, d, 2 * WIDE), BF16),
+            pltpu.VMEM((4, WIDE, d), BF16),
             pltpu.VMEM((SLOTS, 2, d, WIDE), BF16),
             pltpu.VMEM((DN_SLOTS, n, STRIP, d), BF16),
             pltpu.VMEM((SLOTS, 2, 2, hops, rows, WIDE), BF16),
-            pltpu.VMEM((DN_SLOTS, 2, 2, hops, STRIP // 2, d), BF16),
-            dma((2, 6)),
-            dma((11,)),
+            pltpu.VMEM((2, 2, 2, hops, STRIP // 2, d), BF16),
+            dma((4, 6)),
+            dma((15,)),
             dma((SLOTS, 2, 2)),
             dma((SLOTS, 2, 2, hops)),
-            dma((DN_SLOTS, 2, 2)),
-            dma((DN_SLOTS, 2, 2, hops)),
+            dma((2, 2, 2)),
+            dma((2, 2, 2, hops)),
             dma((chunks, 2, 2)),
             dma((chunks, 2, 2, hops)),
         ],
-        compiler_params=pltpu.CompilerParams(collective_id=0, has_side_effects=True, vmem_limit_bytes=33 * 2**20),
+        compiler_params=pltpu.CompilerParams(collective_id=0, has_side_effects=True, vmem_limit_bytes=73 * 2**19),
     )(x, dy, *arrays)
     return pl.pallas_call(
         put,
@@ -429,7 +452,7 @@
         out_shape=[jax.ShapeDtypeStruct(a.shape, a.dtype) for a in made],
         in_specs=[pl.BlockSpec(memory_space=pltpu.VMEM)] * 9,
         out_specs=[anywhere] * 9,
-        scratch_shapes=[dma((9,))],
+        scratch_shapes=[dma((9, layers))],
         compiler_params=pltpu.CompilerParams(vmem_limit_bytes=2**20),
     )(*(pltpu.with_memory_space_constraint(a, pltpu.VMEM) for a in made))
 

time: 414 us -> 411 us (level)
  no operation moved by 1% of the time
where the time goes in v4:
time: 411 us
  Pallas kernels  410 us (100%)
    pallas_call x1, Pallas kernels, device_step(): pl.pallas_call(functools.partial(kernel, n), name='step', out_shape=[pltp...  400 us
    pallas_call x1, Pallas kernels, device_step(): pl.pallas_call(put, name='put', out_shape=[jax.ShapeDtypeStruct(a.shape,...  9.5 us

profile of v4, /device:TPU:21, one launch (start us, length us, event | category | flops | bytes accessed | tf_op | source)
XLA Modules:
  0.0 410.6 jit_solution(4540729456016396601)
XLA Ops:
  0.6 400.3 %step.1 = (bf16[2,512,3072]{2,1,0:T(8,128)(2,1)S(1)}, bf16[2,512,3072]{2,1,0:T(8,128)(2,1)S(1)}, bf16[2,3072,512]{2,1,0:T(8,128)(2,1)S(1)}, f32[2,64,3072]{2,1,0...) custom-call(bf16[1,2048,512]{2,1,0:T(8,128)(2,1)} %x.1, ...), custom_call_target="tpu_custom_call" | custom-call | tf_op jit(solution)/shard_map/step/pallas_call | solution.py:418
  400.9 9.5 %put.1 = (bf16[2,512,3072]{2,1,0:T(8,128)(2,1)}, bf16[2,512,3072]{2,1,0:T(8,128)(2,1)}, bf16[2,3072,512]{2,1,0:T(8,128)(2,1)}, f32[2,64,3072]{2,1,0:T(8,128)}, f...) custom-call(bf16[2,512,3072]{2,1,0:T(8,128)(2,1)S(1)} %get-tuple-ele, ...), custom_call_target="tpu_custom_call" | custom-call | tf_op jit(solution)/shard_map/put/pallas_call | solution.py:449

commit v5 on v4

--- a/solution.py
+++ b/solution.py
@@ -20,6 +20,8 @@
 STEPS = len(GROUPS)
 GU_FROM = 2
 DN_FROM = 3
+EARLY = 4
+EARLY_LAG = 3
 
 
 def dot(a, b, dims=((1,), (0,))):
@@ -217,27 +219,29 @@
                     def _():
                         new_ended(c, e, direction, hop - 1)
 
-                for direction in range(2):
-
                     @pl.when(hop < length(e, direction))
                     def _():
                         new_copies(c, e, direction, hop)
 
-    def pump(t, step):
-        for hop in range(longer + 1):
-            since, due = divmod(GU_FROM + LAG * hop, STEPS)
-            if due == step:
-
-                @pl.when((t >= since) & (t < tiles + since))
-                def _():
-                    gu_event(t - since, hop)
-
-            since, due = divmod(DN_FROM + LAG * hop, STEPS)
-            if due == step:
-
-                @pl.when((t >= since) & (t < tiles + since) & (lax.rem(t - since + 1, per_chunk) == 0))
-                def _():
-                    dn_event(lax.div(t - since, per_chunk), hop)
+    def pump(t, step, early=False):
+        groups = [(LAG, EARLY, tiles)]
+        if early:
+            groups.insert(0, (EARLY_LAG, 0, EARLY))
+        for lag, begin, end in groups:
+            for hop in range(longer + 1):
+                since, due = divmod(GU_FROM + lag * hop, STEPS)
+                if due == step:
+
+                    @pl.when((t >= begin + since) & (t < end + since))
+                    def _():
+                        gu_event(t - since, hop)
+
+                since, due = divmod(DN_FROM + lag * hop, STEPS)
+                if due == step:
+
+                    @pl.when((t >= begin + since) & (t < end + since) & (lax.rem(t - since + 1, per_chunk) == 0))
+                    def _():
+                        dn_event(lax.div(t - since, per_chunk), hop)
 
     def normalise(b, _, turned=True):
         r = pl.ds(aligned(b * few, few), few)
@@ -339,7 +343,7 @@
         work += [functools.partial(da, b) for b in range(4)]
         for step in range(STEPS):
             if not first:
-                pump(t, step)
+                pump(t, step, with_da)
             elif step == GU_FROM:
                 gu_event(0, 0)
             for k in GROUPS[step]:

time: 411 us -> 410 us (level)
  no operation moved by 1% of the time
where the time goes in v5:
time: 410 us
  Pallas kernels  409 us (100%)
    pallas_call x1, Pallas kernels, device_step(): pl.pallas_call(functools.partial(kernel, n), name='step', out_shape=[pltp...  400 us
    pallas_call x1, Pallas kernels, device_step(): pl.pallas_call(put, name='put', out_shape=[jax.ShapeDtypeStruct(a.shape,...  9.5 us

profile of v5, /device:TPU:21, one launch (start us, length us, event | category | flops | bytes accessed | tf_op | source)
XLA Modules:
  0.0 410.3 jit_solution(7437835192878917103)
XLA Ops:
  0.6 399.9 %step.1 = (bf16[2,512,3072]{2,1,0:T(8,128)(2,1)S(1)}, bf16[2,512,3072]{2,1,0:T(8,128)(2,1)S(1)}, bf16[2,3072,512]{2,1,0:T(8,128)(2,1)S(1)}, f32[2,64,3072]{2,1,0...) custom-call(bf16[1,2048,512]{2,1,0:T(8,128)(2,1)} %x.1, ...), custom_call_target="tpu_custom_call" | custom-call | tf_op jit(solution)/shard_map/step/pallas_call | solution.py:422
  400.6 9.5 %put.1 = (bf16[2,512,3072]{2,1,0:T(8,128)(2,1)}, bf16[2,512,3072]{2,1,0:T(8,128)(2,1)}, bf16[2,3072,512]{2,1,0:T(8,128)(2,1)}, f32[2,64,3072]{2,1,0:T(8,128)}, f...) custom-call(bf16[2,512,3072]{2,1,0:T(8,128)(2,1)S(1)} %get-tuple-ele, ...), custom_call_target="tpu_custom_call" | custom-call | tf_op jit(solution)/shard_map/put/pallas_call | solution.py:453
